TPU v7x, 256 devices: a whole 4x4x8 slice. The times are simulated.
256 devices in a mesh: dp: 128 (over y, x_hi, z, core), tensor: 2 (over x_lo).
Axes of the slice: x: 4 (x_hi: 2, x_lo: 2; x = x_hi * 2 + x_lo), y: 4, z: 8, core: 2. Of those that a mesh axis runs over, the one named last changes fastest.
Arguments:
- query_feats: bfloat16 [32768, 768], P('dp'), may hold values from -24 to 24
- key_feats: bfloat16 [512, 768], P('dp'), may hold values from -6 to 6
- key_task: int32 [512], P('dp'), may hold values from 0 to 3
- positive: int32 [32768], P('dp'), may hold values from 0 to 511
- head_weights: bfloat16 [4, 768, 768], P(None, None, 'tensor'), may hold values from -0.21875 to 0.21875
- task_scale: float32 [4], replicated, may hold values from 10 to 30
Outputs:
- query_loss: float32 [32768], P(('dp', 'tensor'))
- weight_grad: float32 [4, 768, 768], P(None, 'dp', 'tensor')
All inputs are finite; a program needn't handle non-finite values.
Results may differ from a plain program's by a relative error of at most 0.0075.
Values may be sent and summed in bfloat16 or wider, within the bound.
No kernel may reach another device: no remote copies, remote signals or barrier semaphores. Data moves between devices by JAX's collectives and lax.ppermute only.
A program may use at most 64 MiB of HBM per device.

v0:
```python
import jax
import jax.numpy as jnp
from jax import lax
from jax.sharding import Mesh
from jax.sharding import PartitionSpec as P

DP = ("dp_0", "dp_1", "dp_2", "dp_3")
DP_TENSOR = ("dp_0", "dp_1", "dp_2", "dp_3", "tensor")


EPS = 1e-06


def from_everyone(x, axis):
    devices = lax.axis_size(axis)
    return lax.all_to_all(jnp.broadcast_to(x[None], (devices, *x.shape)), axis, 0, 0, tiled=True)


def laid_out(blocks, dim):
    blocks = jnp.moveaxis(blocks, 0, dim)
    shape = blocks.shape
    return blocks.reshape(*shape[:dim], shape[dim] * shape[dim + 1], *shape[dim + 2 :])


def gathered_by_axis(x, axes, dim):
    far, near = axes
    initial = from_everyone(x, far)
    blocks = jnp.swapaxes(from_everyone(initial, near), 0, 1)
    return laid_out(blocks.reshape(-1, *x.shape), dim)


def over_copies(x, axis):
    return from_everyone(x, axis).sum(axis=0)


def together(arrays, axis):
    line, at, gathered = (jnp.concatenate([a.reshape(-1) for a in arrays]), 0, [])
    total = over_copies(line, axis)
    for a in arrays:
        gathered.append(total[at : at + a.size].reshape(a.shape))
        at += a.size
    return tuple(gathered)


def in_blocks(x, dim, devices):
    before, after = (x.shape[:dim], x.shape[dim + 1 :])
    return jnp.moveaxis(x.reshape(*before, devices, -1, *after), dim, 0)


def sent_and_summed(x, axis, dim):
    blocks = in_blocks(x, dim, lax.axis_size(axis))
    arrived = lax.all_to_all(blocks, axis, split_axis=0, concat_axis=0, tiled=True)
    return arrived.sum(axis=0)


def gathered_copies(x, axis, dim):
    return laid_out(from_everyone(x, axis), dim)


def summed_rows(x, axes, dim):
    far, near = axes
    own = sent_and_summed(in_blocks(x, dim, lax.axis_size(far)), near, dim + 1)
    return jnp.sum(lax.all_to_all(own, far, 0, 0, tiled=True), axis=0)


def project(rows, task, weights):
    out = jnp.zeros((rows.shape[0], weights.shape[2]), jnp.float32)
    for k in range(weights.shape[0]):
        proj = jnp.dot(rows, weights[k], preferred_element_type=jnp.float32)
        out = jnp.where((task == k)[:, None], proj, out)
    return out.astype(jnp.bfloat16)


def collect(rows, task, grads, n_tasks):
    parts = []
    for k in range(n_tasks):
        masked = jnp.where((task == k)[:, None], grads, jnp.zeros_like(grads))
        parts.append(
            lax.dot_general(
                rows, masked, (((0,), (0,)), ((), ())), preferred_element_type=jnp.float32
            )
        )
    return jnp.stack(parts)


def back_with(proj, inverse, grad, inner):
    values = proj.astype(jnp.float32)
    return (inverse[:, None] * grad - (inverse**3)[:, None] * values * inner[:, None]).astype(
        jnp.bfloat16
    )


def contrast(dots, scale_rows, task_rows, pos_rows, tasks_all):
    scores = dots * scale_rows[:, None]
    same = task_rows[:, None] == tasks_all[None, :]
    expo = jnp.exp(scores)
    expo = jnp.where(same, expo, jnp.zeros_like(expo))
    total = jnp.sum(expo, 1)
    chosen = pos_rows[:, None] == lax.broadcasted_iota(jnp.int32, scores.shape, 1)
    loss = jnp.log(total) - jnp.sum(jnp.where(chosen, scores, jnp.zeros_like(scores)), 1)
    target = jnp.where(chosen, jnp.ones_like(scores), jnp.zeros_like(scores))
    grads = (scale_rows[:, None] * (expo / total[:, None] - target)).astype(jnp.bfloat16)
    return (loss, grads)


def per_device(query_feats, key_feats, key_task, positive, head_weights, task_scale):
    groups = lax.axis_size("tensor")
    member = lax.axis_index("tensor")
    n_tasks = head_weights.shape[0]
    n_query = query_feats.shape[0]
    tasks_all = gathered_by_axis(key_task, (("dp_0", "dp_1", "dp_2"), "dp_3"), 0)
    keys_total = tasks_all.shape[0]
    hits = positive[:, None] == lax.broadcasted_iota(jnp.int32, (n_query, keys_total), 1)
    query_task = jnp.sum(jnp.where(hits, tasks_all[None, :], 0), 1)
    table = query_task[:, None] == lax.broadcasted_iota(jnp.int32, (n_query, n_tasks), 1)
    query_scale = jnp.sum(jnp.where(table, task_scale[None, :], 0.0), 1)
    query_proj = project(query_feats, query_task, head_weights)
    key_proj = project(key_feats, key_task, head_weights)
    own = n_query // groups
    first = member * own
    pos_rows = lax.dynamic_slice_in_dim(positive, first, own)
    task_rows = lax.dynamic_slice_in_dim(query_task, first, own)
    scale_rows = lax.dynamic_slice_in_dim(query_scale, first, own)
    query_values = query_proj.astype(jnp.float32)
    key_values = key_proj.astype(jnp.float32)
    query_sq, key_sq = together(
        (jnp.sum(query_values * query_values, 1), jnp.sum(key_values * key_values, 1)), "tensor"
    )
    query_inv = 1.0 / jnp.sqrt(query_sq + EPS)
    key_inv = 1.0 / jnp.sqrt(key_sq + EPS)
    query_unit = (query_values * query_inv[:, None]).astype(jnp.bfloat16)
    key_unit = (key_values * key_inv[:, None]).astype(jnp.bfloat16)
    keys_cols = gathered_by_axis(key_unit, (("dp_0", "dp_1", "dp_2"), "dp_3"), 0)
    picked = query_unit
    dots = sent_and_summed(
        lax.dot_general(
            picked, keys_cols, (((1,), (1,)), ((), ())), preferred_element_type=jnp.float32
        ),
        "tensor",
        0,
    )
    query_loss, grads = contrast(dots, scale_rows, task_rows, pos_rows, tasks_all)
    piece = gathered_copies(grads, "tensor", 0)
    image = jnp.dot(piece, keys_cols, preferred_element_type=jnp.float32)
    picked = query_unit
    key_acc = lax.dot_general(
        piece, picked, (((0,), (0,)), ((), ())), preferred_element_type=jnp.float32
    )
    key_back = summed_rows(key_acc, (("dp_0", "dp_1", "dp_2"), "dp_3"), 0)
    query_inner, key_inner = together(
        (jnp.sum(query_values * image, 1), jnp.sum(key_values * key_back, 1)), "tensor"
    )
    query_grad = back_with(query_proj, query_inv, image, query_inner)
    key_grad = back_with(key_proj, key_inv, key_back, key_inner)
    weight_terms = collect(query_feats, query_task, query_grad, n_tasks) + collect(
        key_feats, key_task, key_grad, n_tasks
    )
    weight_grad = summed_rows(weight_terms, (("dp_0", "dp_1", "dp_2"), "dp_3"), 1)
    return (query_loss, weight_grad)


def solution(mesh):
    split = Mesh(
        mesh.devices.reshape(4, 2, 8, 2, mesh.shape["tensor"]),
        ("dp_0", "dp_1", "dp_2", "dp_3", "tensor"),
    )
    return jax.shard_map(
        per_device,
        mesh=split,
        in_specs=(P(DP, None), P(DP, None), P(DP), P(DP), P(None, None, "tensor"), P()),
        out_specs=(P(DP_TENSOR), P(None, DP, "tensor")),
        check_vma=False,
    )
```

profile of v0, /device:TPU:2, one launch (start us, length us, event | category | flops | bytes accessed | tf_op | source)
XLA Modules:
  0.0 253.8 jit_solution(17269825557406315172)
XLA Ops:
  0.7 1.4 broadcast_in_dim.187
  2.1 13.7 %all-to-all-start = ((s32[64,1,4]{2,1,0:T(1,128)}), s32[64,1,4]{2,1,0:T(1,128)S(1)}, u32[]{:S(2)}, u32[]{:S(2)}) async-start(s32[64,1,4]{2,1,0:T(1,128)} %broadcast_in_dim.187), calls=%async_computation | async-start | bytes 65536 | tf_op jit(solution)/shard_map/all_to_all | solution.py:16
  15.8 0.7 broadcast_compare_fusion.7
  16.4 1.2 fusion.11
  17.7 1.3 fusion.18
  19.0 1.4 fusion.13
  20.5 0.4 fusion.16
  21.0 0.3 multiply_reduce_fusion.3
  21.4 6.3 %all-to-all-done = s32[64,1,4]{2,1,0:T(1,128)S(1)} async-done(((s32[64,1,4]{2,1,0:T(1,128)}), s32[64,1,4]{2,1,0:T(1,128)S(1)}, u32[]{:S(2)}, u32[]{:S(2)}) %all-to-all-start) | async-done | bytes 1056 | tf_op jit(solution)/shard_map/all_to_all | solution.py:16
  27.8 3.7 %all_to_all.63 = s32[2,1,256]{2,1,0:T(1,128)S(1)} all-to-all(s32[2,1,256]{2,1,0:T(1,128)S(1)} %reshape.165), channel_id=1, replica_groups=mesh['dp_0'=4,'dp_1'=2,'dp_2'=8,'dp_3'=2,'tensor'=2] {'dp_3'}, dimensions={0} | all-to-all | bytes 4096 | tf_op jit(solution)/shard_map/all_to_all | solution.py:16
  31.5 0.5 broadcast.196
  32.0 0.7 reduce.2
  33.2 0.4 fusion.2
  33.6 0.4 multiply_reduce_fusion.1
  34.1 5.5 %all_to_all.64 = f32[2,1,260]{2,1,0:T(1,128)S(1)} all-to-all(f32[2,1,260]{2,1,0:T(1,128)S(1)} %broadcast_in_dim.203), channel_id=1, replica_groups=mesh['dp_0'=4,'dp_1'=2,'dp_2'=8,'dp_3'=2,'tensor'=2] {'tensor'}, dimensions={0} | all-to-all | bytes 4160 | tf_op jit(solution)/shard_map/all_to_all | solution.py:16
  39.8 0.7 broadcast_in_dim.204
  40.5 5.9 %all-to-all-start.3 = ((bf16[64,4,384]{2,1,0:T(4,128)(2,1)}), bf16[64,4,384]{2,1,0:T(4,128)(2,1)S(1)}, u32[]{:S(2)}, u32[]{:S(2)}) async-start(bf16[64,4,384]{2,1,0:T(4,128)(2,1)} %broadcast_in_dim.204), calls=%async_computation.3 | async-start | bytes 393216 | tf_op jit(solution)/shard_map/all_to_all | solution.py:16
  46.5 13.3 %all-to-all-done.3 = bf16[64,4,384]{2,1,0:T(4,128)(2,1)S(1)} async-done(((bf16[64,4,384]{2,1,0:T(4,128)(2,1)}), bf16[64,4,384]{2,1,0:T(4,128)(2,1)S(1)}, u32[]{:S(2)}, u32[]{:S(2)}) %all-to-all-start.3) | async-done | bytes 196640 | tf_op jit(solution)/shard_map/all_to_all | solution.py:16
  60.0 4.0 %all_to_all.65 = bf16[2,64,4,384]{3,2,1,0:T(4,128)(2,1)S(1)} all-to-all(bf16[2,64,4,384]{3,2,1,0:T(4,128)(2,1)S(1)} %broadcast_in_dim.205), channel_id=1, replica_groups=mesh['dp_0'=4,'dp_1'=2,'dp_2'=8,'dp_3'=2,'tensor'=2] {'dp_3'}, dimensions={0} | all-to-all | bytes 786432 | tf_op jit(solution)/shard_map/all_to_all | solution.py:16
  64.3 1.1 fusion.64
  65.4 5.9 %all-to-all-start.5 = ((f32[2,128,512]{2,1,0:T(8,128)}), f32[2,128,512]{2,1,0:T(8,128)S(1)}, u32[]{:S(2)}, u32[]{:S(2)}) async-start(f32[2,128,512]{2,1,0:T(8,128)} %fusion.64), calls=%async_computation.5 | async-start | bytes 1048576 | tf_op jit(solution)/shard_map/all_to_all | solution.py:52
  71.6 6.5 %all-to-all-done.5 = f32[2,128,512]{2,1,0:T(8,128)S(1)} async-done(((f32[2,128,512]{2,1,0:T(8,128)}), f32[2,128,512]{2,1,0:T(8,128)S(1)}, u32[]{:S(2)}, u32[]{:S(2)}) %all-to-all-start.5) | async-done | bytes 524320 | tf_op jit(solution)/shard_map/all_to_all | solution.py:52
  78.8 7.3 %all_to_all.66 = bf16[2,128,512]{1,2,0:T(8,128)(2,1)S(1)} all-to-all(bf16[2,128,512]{1,2,0:T(8,128)(2,1)S(1)} %broadcast_in_dim.209), channel_id=1, replica_groups=mesh['dp_0'=4,'dp_1'=2,'dp_2'=8,'dp_3'=2,'tensor'=2] {'tensor'}, dimensions={0} | all-to-all | bytes 524288 | tf_op jit(solution)/shard_map/all_to_all | solution.py:16
  86.4 0.3 convolution_bitcast_fusion.8
  86.7 4.4 %all_to_all.67 = f32[2,64,4,384]{3,1,2,0:T(8,128)S(1)} all-to-all(f32[2,64,4,384]{3,1,2,0:T(8,128)S(1)} %convolution_bitcast_fusion.8), channel_id=1, replica_groups=mesh['dp_0'=4,'dp_1'=2,'dp_2'=8,'dp_3'=2,'tensor'=2] {'dp_3'}, dimensions={0} | all-to-all | bytes 1572864 | tf_op jit(solution)/shard_map/all_to_all | solution.py:52
  91.1 1.0 copy.102
  92.1 4.6 %all-to-all-start.8 = ((f32[64,4,384]{2,1,0:T(4,128)}), f32[64,4,384]{2,1,0:T(4,128)S(1)}, u32[]{:S(2)}, u32[]{:S(2)}) async-start(f32[64,4,384]{2,1,0:T(4,128)} %copy.102), calls=%async_computation.8 | async-start | bytes 786432 | tf_op jit(solution)/shard_map/all_to_all | solution.py:63
  96.9 0.4 multiply_reduce_fusion
  97.2 17.7 %all-to-all-done.8 = f32[64,4,384]{2,1,0:T(4,128)S(1)} async-done(((f32[64,4,384]{2,1,0:T(4,128)}), f32[64,4,384]{2,1,0:T(4,128)S(1)}, u32[]{:S(2)}, u32[]{:S(2)}) %all-to-all-start.8) | async-done | bytes 393248 | tf_op jit(solution)/shard_map/all_to_all | solution.py:63
  115.2 6.3 %all_to_all.68 = f32[2,1,260]{2,1,0:T(1,128)S(1)} all-to-all(f32[2,1,260]{2,1,0:T(1,128)S(1)} %broadcast_in_dim.210), channel_id=1, replica_groups=mesh['dp_0'=4,'dp_1'=2,'dp_2'=8,'dp_3'=2,'tensor'=2] {'tensor'}, dimensions={0} | all-to-all | bytes 4160 | tf_op jit(solution)/shard_map/all_to_all | solution.py:16
  121.7 0.5 convolution_bitcast_fusion.4
  122.1 0.5 convolution_bitcast_fusion.5
  122.6 1.5 convolution_bitcast_fusion.6
  124.0 1.5 convolution_bitcast_fusion.7
  125.6 1.5 convolution_bitcast_fusion
  127.0 1.5 convolution_bitcast_fusion.1
  128.5 1.5 convolution_bitcast_fusion.2
  130.0 1.6 convolution_bitcast_fusion.3
  131.6 1.4 copy.107
  133.0 1.4 stack.33
  134.3 1.4 copy.106
  135.7 1.4 stack.32
  137.1 2.7 %copy.105 = f32[768,384]{1,0:T(8,128)} copy(f32[768,384]{0,1:T(8,128)} %convolution_bitcast_fusion.6) | data formatting | bytes 2359296 | tf_op jit(solution)/shard_map/dot_general | solution.py:79
  139.8 2.4 stack.31
  142.2 2.7 %copy.104 = f32[768,384]{1,0:T(8,128)} copy(f32[768,384]{0,1:T(8,128)} %convolution_bitcast_fusion.7) | data formatting | bytes 2359296 | tf_op jit(solution)/shard_map/dot_general | solution.py:79
  144.9 2.4 stack.30
  147.3 2.7 %copy.111 = f32[768,384]{1,0:T(8,128)} copy(f32[768,384]{0,1:T(8,128)} %convolution_bitcast_fusion) | data formatting | bytes 2359296 | tf_op jit(solution)/shard_map/dot_general | solution.py:79
  150.0 2.4 stack.38
  152.4 2.7 %copy.110 = f32[768,384]{1,0:T(8,128)} copy(f32[768,384]{0,1:T(8,128)} %convolution_bitcast_fusion.1) | data formatting | bytes 2359296 | tf_op jit(solution)/shard_map/dot_general | solution.py:79
  155.1 2.5 stack.37
  157.6 2.7 %copy.109 = f32[768,384]{1,0:T(8,128)} copy(f32[768,384]{0,1:T(8,128)} %convolution_bitcast_fusion.2) | data formatting | bytes 2359296 | tf_op jit(solution)/shard_map/dot_general | solution.py:79
  160.2 2.4 stack.36
  162.7 2.6 %copy.108 = f32[768,384]{1,0:T(8,128)} copy(f32[768,384]{0,1:T(8,128)} %convolution_bitcast_fusion.3) | data formatting | bytes 2359296 | tf_op jit(solution)/shard_map/dot_general | solution.py:79
  165.3 2.5 stack.35
  167.8 4.1 %fusion = f32[64,4,12,384]{3,2,0,1:T(8,128)S(1)} fusion(f32[1,64,12,384]{3,2,1,0:T(8,128)S(1)} %stack.33, f32[1,64,12,384]{3,2,1,0:T(8,128)S(1)} %stack.32, f32[1,64,12,384]{3,2,1,0:T(8,128)} %stack.31, f32[1,64,12,384]{3,2,1,0:T(8,128)} %stack.30, f32[1,64,12,384]{3,2,1,0:T(8,128)} %stack.38, f32[1,64,12,384]{3,2,1,0:T(8,128)} %stack.37, ...), kind=kLoop, calls=%fused_computation.1 | loop fusion | flops 8257536 | bytes 14155776 | tf_op jit(solution)/shard_map/transpose | solution.py:47
  171.9 1.4 copy.112
  173.4 0.5 copy.113
  173.9 8.6 %all_to_all.69 = f32[2,64,4,6,384]{4,1,3,2,0:T(8,128)} all-to-all(f32[2,64,4,6,384]{4,1,3,2,0:T(8,128)S(1)} %copy.113), channel_id=1, replica_groups=mesh['dp_0'=4,'dp_1'=2,'dp_2'=8,'dp_3'=2,'tensor'=2] {'dp_3'}, dimensions={0} | all-to-all | bytes 9437184 | tf_op jit(solution)/shard_map/all_to_all | solution.py:52
  182.5 2.9 %reduce_sum.148 = f32[64,4,6,384]{3,0,2,1:T(8,128)S(1)} reduce(f32[2,64,4,6,384]{4,1,3,2,0:T(8,128)} %all_to_all.69, f32[]{:T(128)} %constant.18.clone.1), dimensions={0}, to_apply=%region_13.14 | reduce | flops 589824 | bytes 7077892 | tf_op jit(solution)/shard_map/reduce_sum | solution.py:53
  185.4 2.9 %copy.115 = f32[64,4,6,384]{3,1,2,0:T(4,128)} copy(f32[64,4,6,384]{3,0,2,1:T(8,128)S(1)} %reduce_sum.148) | data formatting | bytes 4718592 | tf_op jit(solution)/shard_map/reduce_sum | solution.py:53
  188.4 4.8 %all-to-all-start.11 = ((f32[64,4,6,384]{3,1,2,0:T(4,128)}), f32[64,4,6,384]{3,1,2,0:T(4,128)S(1)}, u32[]{:S(2)}, u32[]{:S(2)}) async-start(f32[64,4,6,384]{3,1,2,0:T(4,128)} %copy.115), calls=%async_computation.11 | async-start | bytes 4718592 | tf_op jit(solution)/shard_map/all_to_all | solution.py:63
  193.2 0.5 log_subtract_fusion
  193.8 59.0 %all-to-all-done.11 = f32[64,4,6,384]{3,1,2,0:T(4,128)S(1)} async-done(((f32[64,4,6,384]{3,1,2,0:T(4,128)}), f32[64,4,6,384]{3,1,2,0:T(4,128)S(1)}, u32[]{:S(2)}, u32[]{:S(2)}) %all-to-all-start.11) | async-done | bytes 2359328 | tf_op jit(solution)/shard_map/all_to_all | solution.py:63
  252.8 1.0 reduce_sum.149
  (55 shorter events, 3.4 us)
Async XLA Ops:
  0.6 18.4 %copy-start = (bf16[256,768]{1,0:T(8,128)(2,1)S(1)}, bf16[256,768]{1,0:T(8,128)(2,1)}, u32[]{:S(2)}) copy-start(bf16[256,768]{1,0:T(8,128)(2,1)} %param.6) | copy-start | bytes 1179652
  0.6 19.8 %copy-start.2 = (bf16[4,768,384]{2,1,0:T(8,128)(2,1)S(1)}, bf16[4,768,384]{2,1,0:T(8,128)(2,1)}, u32[]{:S(2)}) copy-start(bf16[4,768,384]{2,1,0:T(8,128)(2,1)} %param.10) | copy-start | bytes 7077892
  2.1 25.5 %all-to-all-start = ((s32[64,1,4]{2,1,0:T(1,128)}), s32[64,1,4]{2,1,0:T(1,128)S(1)}, u32[]{:S(2)}, u32[]{:S(2)}) async-start(s32[64,1,4]{2,1,0:T(1,128)} %broadcast_in_dim.187), calls=%async_computation | async-start | bytes 65536 | tf_op jit(solution)/shard_map/all_to_all | solution.py:16
  17.7 3.2 %copy-start.3 = (bf16[4,768]{1,0:T(4,128)(2,1)S(1)}, bf16[4,768]{1,0:T(4,128)(2,1)}, u32[]{:S(2)}) copy-start(bf16[4,768]{1,0:T(4,128)(2,1)} %param.7) | copy-start | bytes 18436
  20.5 12.5 %copy-start.4 = (s32[256]{0:T(256)S(1)}, s32[256]{0:T(256)}, u32[]{:S(2)}) copy-start(s32[256]{0:T(256)} %param.9) | copy-start | bytes 3076
  40.5 19.4 %all-to-all-start.3 = ((bf16[64,4,384]{2,1,0:T(4,128)(2,1)}), bf16[64,4,384]{2,1,0:T(4,128)(2,1)S(1)}, u32[]{:S(2)}, u32[]{:S(2)}) async-start(bf16[64,4,384]{2,1,0:T(4,128)(2,1)} %broadcast_in_dim.204), calls=%async_computation.3 | async-start | bytes 393216 | tf_op jit(solution)/shard_map/all_to_all | solution.py:16
  64.2 7.3 %copy-start.5 = (f32[4]{0:T(128)S(1)}, f32[4]{0:T(128)}, u32[]{:S(2)}) copy-start(f32[4]{0:T(128)} %param.11) | copy-start | bytes 52
  65.4 12.7 %all-to-all-start.5 = ((f32[2,128,512]{2,1,0:T(8,128)}), f32[2,128,512]{2,1,0:T(8,128)S(1)}, u32[]{:S(2)}, u32[]{:S(2)}) async-start(f32[2,128,512]{2,1,0:T(8,128)} %fusion.64), calls=%async_computation.5 | async-start | bytes 1048576 | tf_op jit(solution)/shard_map/all_to_all | solution.py:52
  92.1 22.8 %all-to-all-start.8 = ((f32[64,4,384]{2,1,0:T(4,128)}), f32[64,4,384]{2,1,0:T(4,128)S(1)}, u32[]{:S(2)}, u32[]{:S(2)}) async-start(f32[64,4,384]{2,1,0:T(4,128)} %copy.102), calls=%async_computation.8 | async-start | bytes 786432 | tf_op jit(solution)/shard_map/all_to_all | solution.py:63
  188.4 64.4 %all-to-all-start.11 = ((f32[64,4,6,384]{3,1,2,0:T(4,128)}), f32[64,4,6,384]{3,1,2,0:T(4,128)S(1)}, u32[]{:S(2)}, u32[]{:S(2)}) async-start(f32[64,4,6,384]{3,1,2,0:T(4,128)} %copy.115), calls=%async_computation.11 | async-start | bytes 4718592 | tf_op jit(solution)/shard_map/all_to_all | solution.py:63
  193.2 60.6 %copy-start.1 = (bf16[256,768]{1,0:T(8,128)(2,1)S(1)}, bf16[256,768]{1,0:T(8,128)(2,1)}, u32[]{:S(2)}) copy-start(bf16[256,768]{1,0:T(8,128)(2,1)} %param.6) | copy-start | bytes 1179652
where the time goes:
time: 255 us; the launch traced here: 254 us
  waiting for transfers between devices  103 us (40%)
  local copies, waits for them, and re-layouts  46.5 us (18%)
  blocking collectives  39.8 us (16%)
  starting transfers between devices  35 us (14%)
  matrix products  17.3 us (7%)
  other arithmetic  11.4 us (4%)
    all_to_all x2, waiting for transfers between devices, summed_rows(): return jnp.sum(lax.all_to_all(own, far, 0, 0, tiled=True), axis=0)  76.7 us
    all_to_all x5, blocking collectives, from_everyone(): lax.all_to_all(jnp.broadcast_to(x[None], (devices, *x.shape)), axis, 0, 0...  26.9 us
    all_to_all x2, waiting for transfers between devices, from_everyone(): lax.all_to_all(jnp.broadcast_to(x[None], (devices, *x.shape)), axis, 0, 0...  19.6 us
    all_to_all x2, starting transfers between devices, from_everyone(): lax.all_to_all(jnp.broadcast_to(x[None], (devices, *x.shape)), axis, 0, 0...  19.6 us
    dot_general x8, local copies, waits for them, and re-layouts, collect(): lax.dot_general(rows, masked, (((0,), (0,)), ((), ())), preferred_element...  18.8 us
    another operation x8, local copies, waits for them, and re-layouts, collect(): return jnp.stack(parts)  17.4 us
    all_to_all x2, blocking collectives, sent_and_summed(): lax.all_to_all(blocks, axis, split_axis=0, concat_axis=0, tiled=True)  13 us
    dot_general x8, matrix products, collect(): lax.dot_general(rows, masked, (((0,), (0,)), ((), ())), preferred_element...  9.81 us
  transfers between devices with their start and end apart: 5, of which 5 were waited for; matrix products, arithmetic and copies ran while one was open for 3% of the time, Pallas kernels for 0%

commit v1 on v0

v1 whole, which is shorter than its diff:
```python
import jax
import jax.numpy as jnp
from jax import lax
from jax.sharding import Mesh
from jax.sharding import PartitionSpec as P

FAR = ("dp_0", "dp_1", "dp_2")
CORE = "dp_3"
DP = FAR + (CORE,)
DP_TENSOR = DP + ("tensor",)
EPS = 1e-06
F32 = jnp.float32
BF16 = jnp.bfloat16


def swapped(x, axis):
    return lax.ppermute(x, axis, [(0, 1), (1, 0)])


def dot(a, b, dims):
    return lax.dot_general(a, b, (dims, ((), ())), preferred_element_type=F32)


def expansion(n_blocks, n_tasks, width, core, depth):
    rows = n_blocks * n_tasks * width
    row = lax.broadcasted_iota(jnp.int32, (rows, 1), 0)
    block, r = row // (n_tasks * width), row % width
    column = (2 * block + core) * width + r
    return (column == lax.broadcasted_iota(jnp.int32, (rows, depth), 1)).astype(BF16)


def by_task(rows, weights):
    return [dot(rows, weights[k], ((1,), (0,))).astype(BF16) for k in range(weights.shape[0])]


def chosen_task(parts, task):
    out = parts[0]
    for k in range(1, len(parts)):
        out = jnp.where((task == k)[:, None], parts[k], out)
    return out


def per_device(query_feats, key_feats, key_task, positive, head_weights, task_scale):
    core, member = lax.axis_index(CORE), lax.axis_index("tensor")
    n_tasks, depth, width = head_weights.shape
    n_query = query_feats.shape[0]
    own = n_query // 2
    n_far = lax.axis_size(FAR)
    per = key_feats.shape[0]
    out_rows = depth // (2 * n_far)

    feats = jnp.concatenate(
        [
            lax.dynamic_slice_in_dim(query_feats, member * own, own),
            lax.dynamic_slice_in_dim(query_feats, (1 - member) * own, own),
        ]
    )
    pos = jnp.concatenate(
        [
            lax.dynamic_slice_in_dim(positive, member * own, own),
            lax.dynamic_slice_in_dim(positive, (1 - member) * own, own),
        ]
    )

    tasks_in = jnp.broadcast_to(key_task.astype(BF16)[:, None], (per, 128))
    sent = jnp.concatenate([key_feats, tasks_in], 1)
    arrived = lax.all_to_all(
        jnp.broadcast_to(sent[None], (n_far, *sent.shape)), FAR, 0, 0, tiled=True
    ).reshape(n_far * per, depth + 128)
    keys = jnp.concatenate([arrived, swapped(arrived, CORE)])
    n_keys = keys.shape[0]
    at = lax.iota(jnp.int32, n_keys)
    half, inside = at // (n_far * per), at % (n_far * per)
    key_core = jnp.where(half == 0, core, 1 - core)
    key_index = (2 * (inside // per) + key_core) * per + inside % per
    all_feats, all_task = keys[:, :depth], keys[:, depth].astype(jnp.int32)

    chosen = pos[:, None] == key_index[None, :]
    query_task = jnp.sum(jnp.where(chosen, all_task[None, :], 0), 1)
    table = query_task[:own, None] == lax.broadcasted_iota(jnp.int32, (own, n_tasks), 1)
    scale = jnp.sum(jnp.where(table, task_scale[None, :], 0.0), 1)

    query_proj = chosen_task(by_task(feats, head_weights), query_task)
    key_proj = chosen_task(by_task(all_feats, head_weights), all_task)
    query_values, key_values = query_proj.astype(F32), key_proj.astype(F32)
    query_sq = jnp.sum(query_values * query_values, 1)
    key_sq = jnp.sum(key_values * key_values, 1)
    dots = dot(query_proj, key_proj, ((1,), (1,)))
    tail = jnp.concatenate(
        [
            key_sq[None, :],
            jnp.pad(query_sq, (0, n_keys - n_query))[None, :],
            jnp.zeros((6, n_keys), F32),
        ]
    )
    got = swapped(jnp.concatenate([dots[own:], tail]), "tensor")
    full = dots[:own] + got[:own]
    key_sq = key_sq + got[own]
    other_sq = got[own + 1, :n_query]
    query_sq = query_sq + jnp.concatenate([other_sq[own:], other_sq[:own]])
    query_inv = 1.0 / jnp.sqrt(query_sq + EPS)
    key_inv = 1.0 / jnp.sqrt(key_sq + EPS)

    half_cos = full * key_inv[None, :]
    scores = half_cos * (scale * query_inv[:own])[:, None]
    same = query_task[:own, None] == all_task[None, :]
    expo = jnp.where(same, jnp.exp(scores), 0.0)
    total = jnp.sum(expo, 1)
    target = chosen[:own]
    query_loss = jnp.log(total) - jnp.sum(jnp.where(target, scores, 0.0), 1)
    grads = (scale[:, None] * (expo / total[:, None] - target.astype(F32))).astype(BF16)
    wide = grads.astype(F32)
    query_inner = jnp.sum(wide * half_cos, 1)
    key_inner = jnp.sum(wide * full * query_inv[:own, None], 0)
    inner = jnp.stack([key_inner, jnp.pad(query_inner, (0, n_keys - own))])
    high = inner.astype(BF16)
    low = (inner - high.astype(F32)).astype(BF16)
    got = swapped(jnp.concatenate([grads, high, low, jnp.zeros((4, n_keys), BF16)]), "tensor")
    both = jnp.concatenate([grads, got[:own]])
    other = got[own : own + 2].astype(F32) + got[own + 2 : own + 4].astype(F32)
    key_inner = key_inner + other[0]
    query_inner = jnp.concatenate([query_inner, other[1, :own]])

    query_unit = (query_values * query_inv[:, None]).astype(BF16)
    key_unit = (key_values * key_inv[:, None]).astype(BF16)
    query_back = dot(both, key_unit, ((1,), (0,)))
    key_back = dot(both, query_unit, ((0,), (0,)))

    def through(values, inverse, back, inner):
        return (
            inverse[:, None] * back - (inverse**3)[:, None] * values * inner[:, None]
        ).astype(BF16)

    back = jnp.concatenate(
        [
            through(query_values, query_inv, query_back, query_inner),
            through(key_values, key_inv, key_back, key_inner),
        ]
    )

    row_feats = jnp.concatenate([feats, all_feats])
    row_task = jnp.concatenate([query_task, all_task])

    def share(of_core):
        spread = dot(
            expansion(n_far, n_tasks, out_rows, of_core, depth), row_feats, ((1,), (1,))
        ).astype(BF16)
        line_task = lax.iota(jnp.int32, spread.shape[0]) % (n_tasks * out_rows) // out_rows
        spread = jnp.where(line_task[:, None] == row_task[None, :], spread, jnp.zeros_like(spread))
        return dot(spread, back, ((1,), (0,)))

    away = share(1 - core).astype(BF16)
    mine = share(core) + swapped(away, CORE).astype(F32)
    blocks = mine.astype(BF16).reshape(n_far, n_tasks * out_rows, width)
    arrived = lax.all_to_all(blocks, FAR, 0, 0, tiled=True)
    weight_grad = jnp.sum(arrived.astype(F32), 0).reshape(n_tasks, out_rows, width)
    return (query_loss, weight_grad)


def solution(mesh):
    split = Mesh(
        mesh.devices.reshape(4, 2, 8, 2, mesh.shape["tensor"]),
        DP_TENSOR,
    )
    return jax.shard_map(
        per_device,
        mesh=split,
        in_specs=(P(DP, None), P(DP, None), P(DP), P(DP), P(None, None, "tensor"), P()),
        out_specs=(P(DP_TENSOR), P(None, DP, "tensor")),
        check_vma=False,
    )
```

time: 255 us -> 110 us (0.43)
  local copies, waits for them, and re-layouts: 46.5 us -> 2.94 us
  blocking collectives: 39.8 us -> 0 us
  waiting for transfers between devices: 103 us -> 64.9 us
  starting transfers between devices: 35 us -> 22 us
  other arithmetic: 11.4 us -> 3.82 us
    all_to_all x5 -> x2, waiting for transfers between devices: 103 us -> 51 us  [the longest x1 33.4 us: per_device(): arrived = lax.all_to_all(blocks, FAR, 0, 0, tiled=True)]
    all_to_all x7 -> x0, blocking collectives: 39.8 us -> none  [the longest x5 26.9 us: from_everyone(): lax.all_to_all(jnp.broadcast_to(x[None], (devices, *x.shape)), axis, 0, 0...]
    dot_general x10 -> x0, local copies, waits for them, and re-layouts: 19 us -> none  [the longest x8 18.8 us: collect(): lax.dot_general(rows, masked, (((0,), (0,)), ((), ())), preferred_element...]
    another operation x10 -> x0, local copies, waits for them, and re-layouts: 17.6 us -> none  [the longest x8 17.4 us: collect(): return jnp.stack(parts)]
    all_to_all x5 -> x2, starting transfers between devices: 35 us -> 18.8 us  [the longest x1 13.7 us: per_device(): lax.all_to_all(jnp.broadcast_to(sent[None], (n_far, *sent.shape)), FAR, 0...]
    ppermute x0 -> x4, waiting for transfers between devices: none -> 13.9 us  [swapped(): return lax.ppermute(x, axis, [(0, 1), (1, 0)])]
    transpose x1 -> x0, other arithmetic: 4.11 us -> none  [in_blocks(): return jnp.moveaxis(x.reshape(*before, devices, -1, *after), dim, 0)]
    reduce_sum x2 -> x0, local copies, waits for them, and re-layouts: 3.92 us -> none  [sent_and_summed(): return arrived.sum(axis=0)]
  transfers between devices with their start and end apart: 5 -> 6, of which waited for: 5 -> 6; matrix products, arithmetic and copies ran while one was open for 3% -> 3% of each run, Pallas kernels for 0% -> 0%
where the time goes in v1:
time: 110 us
  waiting for transfers between devices  64.9 us (59%)
  starting transfers between devices  22 us (20%)
  matrix products  15.2 us (14%)
  other arithmetic  3.82 us (3%)
  local copies, waits for them, and re-layouts  2.94 us (3%)
    all_to_all x1, waiting for transfers between devices, per_device(): arrived = lax.all_to_all(blocks, FAR, 0, 0, tiled=True)  33.4 us
    all_to_all x1, waiting for transfers between devices, per_device(): lax.all_to_all(jnp.broadcast_to(sent[None], (n_far, *sent.shape)), FAR, 0...  17.6 us
    dot_general x13, matrix products, dot(): return lax.dot_general(a, b, (dims, ((), ())), preferred_element_type=F32)  15.2 us
    ppermute x4, waiting for transfers between devices, swapped(): return lax.ppermute(x, axis, [(0, 1), (1, 0)])  13.9 us
    all_to_all x1, starting transfers between devices, per_device(): lax.all_to_all(jnp.broadcast_to(sent[None], (n_far, *sent.shape)), FAR, 0...  13.7 us
    all_to_all x1, starting transfers between devices, per_device(): arrived = lax.all_to_all(blocks, FAR, 0, 0, tiled=True)  5.14 us
    ppermute x4, starting transfers between devices, swapped(): return lax.ppermute(x, axis, [(0, 1), (1, 0)])  3.14 us
  transfers between devices with their start and end apart: 6, of which 6 were waited for; matrix products, arithmetic and copies ran while one was open for 3% of the time, Pallas kernels for 0%

profile of v1, /device:TPU:2, one launch (start us, length us, event | category | flops | bytes accessed | tf_op | source)
XLA Modules:
  0.0 109.7 jit_solution(14559673318330501274)
XLA Ops:
  0.6 0.0 copy-start
  0.6 0.7 convert_element_type.108
  1.3 0.1 broadcast_in_dim.135
  1.4 0.7 pad_maximum_fusion.12
  2.1 0.9 broadcast_in_dim.136
  3.0 13.7 %all-to-all-start = ((bf16[64,4,896]{2,1,0:T(4,128)(2,1)}), bf16[64,4,896]{2,1,0:T(4,128)(2,1)S(1)}, u32[]{:S(2)}, u32[]{:S(2)}) async-start(bf16[64,4,896]{2,1,0:T(4,128)(2,1)} %broadcast_in_dim.136), calls=%async_computation | async-start | bytes 917504 | tf_op jit(solution)/shard_map/all_to_all | solution.py:67
  16.7 0.1 pad.32.clone
  16.8 0.8 fusion.92
  17.6 0.1 broadcast_compare_fusion
  17.8 17.6 %all-to-all-done = bf16[64,4,896]{2,1,0:T(4,128)(2,1)S(1)} async-done(((bf16[64,4,896]{2,1,0:T(4,128)(2,1)}), bf16[64,4,896]{2,1,0:T(4,128)(2,1)S(1)}, u32[]{:S(2)}, u32[]{:S(2)}) %all-to-all-start) | async-done | bytes 458784 | tf_op jit(solution)/shard_map/all_to_all | solution.py:67
  35.4 0.1 reshape.223
  35.5 0.0 copy-start.1
  35.5 0.1 collective-permute-start
  35.6 0.0 copy-done
  35.7 1.6 %convolution_convert_fusion.5 = bf16[256,384]{1,0:T(8,128)(2,1)S(1)} fusion(bf16[4,768,384]{2,1,0:T(8,128)(2,1)} %param.10, bf16[128,768]{1,0:T(8,128)(2,1)S(1)} %get-tuple-element.22, bf16[128,768]{1,0:T(8,128)(2,1)S(1)} %get-tuple-element.21), kind=kOutput, calls=%fused_computation.30 | convolution fusion | flops 151879680 | bytes 1179648 | tf_op jit(solution)/shard_map/dot_general | solution.py:21
  37.3 0.1 collective-permute-done
  37.5 0.1 convert_reduce_fusion.1
  37.6 0.0 copy-done.1
  37.6 0.6 convolution_convert_fusion.1
  38.2 0.3 fusion.44
  38.5 0.2 select_reduce_fusion
  38.7 0.4 fusion.15
  39.1 0.4 fusion.14
  39.5 0.4 fusion.36
  39.9 0.6 fusion.10
  40.5 0.6 fusion.9
  41.1 0.7 fusion.17
  41.8 0.0 copy-start.2
  41.8 0.3 fusion.93
  42.2 0.1 maximum_maximum_fusion
  42.2 1.5 %collective-permute-start.1 = (f32[136,512]{1,0:T(8,128)S(1)}, f32[136,512]{1,0:T(8,128)S(1)}, u32[]{:S(2)}, u32[]{:S(2)}) collective-permute-start(f32[136,512]{1,0:T(8,128)S(1)} %maximum_maximum_fusion), channel_id=1, source_target_pairs={{0,1},{1,0},{2,3},{3,2},{4,5},{5,4},{6,7},{7,6},{8,9},{9,8},{10,11... | collective-permute-start | bytes 835592 | tf_op jit(solution)/shard_map/ppermute | solution.py:17
  43.8 0.1 pad.19.clone
  43.9 0.1 slice.98
  44.0 0.0 copy-done.2
  44.0 0.1 select_reduce_fusion.2
  44.0 7.1 %collective-permute-done.1 = f32[136,512]{1,0:T(8,128)S(1)} collective-permute-done((f32[136,512]{1,0:T(8,128)S(1)}, f32[136,512]{1,0:T(8,128)S(1)}, u32[]{:S(2)}, u32[]{:S(2)}) %collective-permute-start.1) | collective-permute-done | bytes 278560 | tf_op jit(solution)/shard_map/ppermute | solution.py:17
  51.2 0.2 fusion.49
  51.4 0.3 fusion.43
  51.7 0.1 maximum_maximum_fusion.1
  51.8 1.5 %collective-permute-start.2 = (bf16[136,512]{1,0:T(8,128)(2,1)S(1)}, bf16[136,512]{1,0:T(8,128)(2,1)S(1)}, u32[]{:S(2)}, u32[]{:S(2)}) collective-permute-start(bf16[136,512]{1,0:T(8,128)(2,1)S(1)} %maximum_maximum_fusion.1), channel_id=1, source_target_pairs={{0,1},{1,0},{2,3},{3,2},{4,5},{5,4},{6,7},{7,6},{8,9},{9,8},{10,11... | collective-permute-start | bytes 417800 | tf_op jit(solution)/shard_map/ppermute | solution.py:17
  53.4 3.6 %collective-permute-done.2 = bf16[136,512]{1,0:T(8,128)(2,1)S(1)} collective-permute-done((bf16[136,512]{1,0:T(8,128)(2,1)S(1)}, bf16[136,512]{1,0:T(8,128)(2,1)S(1)}, u32[]{:S(2)}, u32[]{:S(2)}) %collective-permute-start.2) | collective-permute-done | bytes 139296 | tf_op jit(solution)/shard_map/ppermute | solution.py:17
  57.0 0.4 fusion.7
  57.5 0.4 fusion.12
  57.9 4.5 %convolution_convert_fusion = bf16[1536,384]{1,0:T(8,128)(2,1)} fusion(s32[1536]{0:T(1024)S(1)} %get-tuple-element.39, s32[768]{0:T(1024)S(1)} %pad_add_fusion, s32[1536]{0:T(1024)S(1)} %get-tuple-element.38, bf16[512,768]{1,0:T(8,128)(2,1)S(1)} %slice.98, bf16[128,768]{1,0:T(8,128)(2,1)S(1)} %get-tuple-element.22, ...), kind=kOutput, calls=%fused_computation.8 | convolution fusion | flops 2727936000 | bytes 2964480 | tf_op jit(solution)/shard_map/dot_general | solution.py:21
  62.4 0.0 collective-permute-start.3
  62.4 3.0 %collective-permute-done.3 = bf16[1536,384]{1,0:T(8,128)(2,1)S(1)} collective-permute-done((bf16[1536,384]{1,0:T(8,128)(2,1)}, bf16[1536,384]{1,0:T(8,128)(2,1)S(1)}, u32[]{:S(2)}, u32[]{:S(2)}) %collective-permute-start.3) | collective-permute-done | bytes 1179680 | tf_op jit(solution)/shard_map/ppermute | solution.py:17
  65.4 4.4 %add_convert_fusion = bf16[1536,384]{1,0:T(8,128)(2,1)} fusion(bf16[1536,384]{1,0:T(8,128)(2,1)S(1)} %collective-permute-done.3, s32[1536]{0:T(1024)S(1)} %fusion.54, s32[768]{0:T(1024)S(1)} %pad_add_fusion, s32[1536]{0:T(1024)S(1)} %get-tuple-element.38, bf16[512,768]{1,0:T(8,128)(2,1)S(1)} %slice.98, bf16[128,768]{1,0:T(8,128)(2,1)S(1)} %get-tuple-element.22, ...), kind=kOutput, calls=%fused_computation.10 | convolution fusion | flops 2729115648 | bytes 4144128 | tf_op jit(solution)/shard_map/dot_general | solution.py:21
  69.8 5.1 %all-to-all-start.1 = ((bf16[64,24,384]{2,1,0:T(8,128)(2,1)}), bf16[64,24,384]{2,1,0:T(8,128)(2,1)S(1)}, u32[]{:S(2)}, u32[]{:S(2)}) async-start(bf16[64,24,384]{2,1,0:T(8,128)(2,1)} %bitcast.14), calls=%async_computation.1 | async-start | bytes 2359296 | tf_op jit(solution)/shard_map/all_to_all | solution.py:155
  74.9 0.5 log_subtract_fusion
  75.5 33.4 %all-to-all-done.1 = bf16[64,24,384]{2,1,0:T(8,128)(2,1)S(1)} async-done(((bf16[64,24,384]{2,1,0:T(8,128)(2,1)}), bf16[64,24,384]{2,1,0:T(8,128)(2,1)S(1)}, u32[]{:S(2)}, u32[]{:S(2)}) %all-to-all-start.1) | async-done | bytes 1179680 | tf_op jit(solution)/shard_map/all_to_all | solution.py:155
  108.9 0.2 convert_reduce_fusion
  109.1 0.6 copy.13
  (29 shorter events, 0.3 us)
Async XLA Ops:
  0.6 35.0 %copy-start = (bf16[256,768]{1,0:T(8,128)(2,1)S(1)}, bf16[256,768]{1,0:T(8,128)(2,1)}, u32[]{:S(2)}) copy-start(bf16[256,768]{1,0:T(8,128)(2,1)} %param.6) | copy-start | bytes 1179652
  3.0 32.4 %all-to-all-start = ((bf16[64,4,896]{2,1,0:T(4,128)(2,1)}), bf16[64,4,896]{2,1,0:T(4,128)(2,1)S(1)}, u32[]{:S(2)}, u32[]{:S(2)}) async-start(bf16[64,4,896]{2,1,0:T(4,128)(2,1)} %broadcast_in_dim.136), calls=%async_computation | async-start | bytes 917504 | tf_op jit(solution)/shard_map/all_to_all | solution.py:67
  35.5 2.1 %copy-start.1 = (bf16[4,768,384]{2,1,0:T(8,128)(2,1)S(1)}, bf16[4,768,384]{2,1,0:T(8,128)(2,1)}, u32[]{:S(2)}) copy-start(bf16[4,768,384]{2,1,0:T(8,128)(2,1)} %param.10) | copy-start | bytes 7077892
  35.5 1.9 %collective-permute-start = (bf16[256,896]{1,0:T(8,128)(2,1)S(1)}, bf16[256,896]{1,0:T(8,128)(2,1)S(1)}, u32[]{:S(2)}, u32[]{:S(2)}) collective-permute-start(bf16[256,896]{1,0:T(8,128)(2,1)S(1)} %reshape.223), channel_id=1, source_target_pairs={{0,2},{2,0},{1,3},{3,1},{4,6},{6,4},{5,7},{7,5},{8,10},{10,8},{9,1... | collective-permute-start | bytes 1376264 | tf_op jit(solution)/shard_map/ppermute | solution.py:17
  41.8 2.2 %copy-start.2 = (f32[4]{0:T(128)S(1)}, f32[4]{0:T(128)}, u32[]{:S(2)}) copy-start(f32[4]{0:T(128)} %param.11) | copy-start | bytes 52
  42.2 8.9 %collective-permute-start.1 = (f32[136,512]{1,0:T(8,128)S(1)}, f32[136,512]{1,0:T(8,128)S(1)}, u32[]{:S(2)}, u32[]{:S(2)}) collective-permute-start(f32[136,512]{1,0:T(8,128)S(1)} %maximum_maximum_fusion), channel_id=1, source_target_pairs={{0,1},{1,0},{2,3},{3,2},{4,5},{5,4},{6,7},{7,6},{8,9},{9,8},{10,11... | collective-permute-start | bytes 835592 | tf_op jit(solution)/shard_map/ppermute | solution.py:17
  51.8 5.1 %collective-permute-start.2 = (bf16[136,512]{1,0:T(8,128)(2,1)S(1)}, bf16[136,512]{1,0:T(8,128)(2,1)S(1)}, u32[]{:S(2)}, u32[]{:S(2)}) collective-permute-start(bf16[136,512]{1,0:T(8,128)(2,1)S(1)} %maximum_maximum_fusion.1), channel_id=1, source_target_pairs={{0,1},{1,0},{2,3},{3,2},{4,5},{5,4},{6,7},{7,6},{8,9},{9,8},{10,11... | collective-permute-start | bytes 417800 | tf_op jit(solution)/shard_map/ppermute | solution.py:17
  62.4 3.1 %collective-permute-start.3 = (bf16[1536,384]{1,0:T(8,128)(2,1)}, bf16[1536,384]{1,0:T(8,128)(2,1)S(1)}, u32[]{:S(2)}, u32[]{:S(2)}) collective-permute-start(bf16[1536,384]{1,0:T(8,128)(2,1)} %convolution_convert_fusion), channel_id=1, source_target_pairs={{0,2},{2,0},{1,3},{3,1},{4,6},{6,4},{5,7},{7,5},{8,10},{10,8},{9,1... | collective-permute-start | bytes 3538952 | tf_op jit(solution)/shard_map/ppermute | solution.py:17
  69.8 39.1 %all-to-all-start.1 = ((bf16[64,24,384]{2,1,0:T(8,128)(2,1)}), bf16[64,24,384]{2,1,0:T(8,128)(2,1)S(1)}, u32[]{:S(2)}, u32[]{:S(2)}) async-start(bf16[64,24,384]{2,1,0:T(8,128)(2,1)} %bitcast.14), calls=%async_computation.1 | async-start | bytes 2359296 | tf_op jit(solution)/shard_map/all_to_all | solution.py:155

commit v2 on v1

--- a/solution.py
+++ b/solution.py
@@ -49,6 +49,17 @@
     per = key_feats.shape[0]
     out_rows = depth // (2 * n_far)
 
+    tasks_in = jnp.broadcast_to(key_task.astype(BF16)[:, None], (per, 128))
+    sent = jnp.concatenate([key_feats, tasks_in], 1)
+    sent, core, member = lax.optimization_barrier((sent, core, member))
+    arrived = lax.all_to_all(
+        jnp.broadcast_to(sent[None], (n_far, *sent.shape)), FAR, 0, 0, tiled=True
+    ).reshape(n_far * per, depth + 128)
+    arrived, query_feats, positive, core, member = lax.optimization_barrier(
+        (arrived, query_feats, positive, core, member)
+    )
+    keys = jnp.concatenate([arrived, swapped(arrived, CORE)])
+
     feats = jnp.concatenate(
         [
             lax.dynamic_slice_in_dim(query_feats, member * own, own),
@@ -62,12 +73,6 @@
         ]
     )
 
-    tasks_in = jnp.broadcast_to(key_task.astype(BF16)[:, None], (per, 128))
-    sent = jnp.concatenate([key_feats, tasks_in], 1)
-    arrived = lax.all_to_all(
-        jnp.broadcast_to(sent[None], (n_far, *sent.shape)), FAR, 0, 0, tiled=True
-    ).reshape(n_far * per, depth + 128)
-    keys = jnp.concatenate([arrived, swapped(arrived, CORE)])
     n_keys = keys.shape[0]
     at = lax.iota(jnp.int32, n_keys)
     half, inside = at // (n_far * per), at % (n_far * per)
@@ -80,19 +85,25 @@
     table = query_task[:own, None] == lax.broadcasted_iota(jnp.int32, (own, n_tasks), 1)
     scale = jnp.sum(jnp.where(table, task_scale[None, :], 0.0), 1)
 
+    row_feats = jnp.concatenate([feats, all_feats])
+    row_task = jnp.concatenate([query_task, all_task])
+
+    def spread(of_core):
+        lines = dot(
+            expansion(n_far, n_tasks, out_rows, of_core, depth), row_feats, ((1,), (1,))
+        ).astype(BF16)
+        line_task = lax.iota(jnp.int32, lines.shape[0]) % (n_tasks * out_rows) // out_rows
+        return jnp.where(line_task[:, None] == row_task[None, :], lines, jnp.zeros_like(lines))
+
+    away_feats, my_feats = lax.optimization_barrier((spread(1 - core), spread(core)))
+
     query_proj = chosen_task(by_task(feats, head_weights), query_task)
     key_proj = chosen_task(by_task(all_feats, head_weights), all_task)
     query_values, key_values = query_proj.astype(F32), key_proj.astype(F32)
     query_sq = jnp.sum(query_values * query_values, 1)
     key_sq = jnp.sum(key_values * key_values, 1)
     dots = dot(query_proj, key_proj, ((1,), (1,)))
-    tail = jnp.concatenate(
-        [
-            key_sq[None, :],
-            jnp.pad(query_sq, (0, n_keys - n_query))[None, :],
-            jnp.zeros((6, n_keys), F32),
-        ]
-    )
+    tail = jnp.stack([key_sq, jnp.tile(query_sq, n_keys // n_query)] * 4)
     got = swapped(jnp.concatenate([dots[own:], tail]), "tensor")
     full = dots[:own] + got[:own]
     key_sq = key_sq + got[own]
@@ -112,10 +123,10 @@
     wide = grads.astype(F32)
     query_inner = jnp.sum(wide * half_cos, 1)
     key_inner = jnp.sum(wide * full * query_inv[:own, None], 0)
-    inner = jnp.stack([key_inner, jnp.pad(query_inner, (0, n_keys - own))])
+    inner = jnp.stack([key_inner, jnp.tile(query_inner, n_keys // own)])
     high = inner.astype(BF16)
     low = (inner - high.astype(F32)).astype(BF16)
-    got = swapped(jnp.concatenate([grads, high, low, jnp.zeros((4, n_keys), BF16)]), "tensor")
+    got = swapped(jnp.concatenate([grads, high, low, high, low]), "tensor")
     both = jnp.concatenate([grads, got[:own]])
     other = got[own : own + 2].astype(F32) + got[own + 2 : own + 4].astype(F32)
     key_inner = key_inner + other[0]
@@ -138,20 +149,11 @@
         ]
     )
 
-    row_feats = jnp.concatenate([feats, all_feats])
-    row_task = jnp.concatenate([query_task, all_task])
-
-    def share(of_core):
-        spread = dot(
-            expansion(n_far, n_tasks, out_rows, of_core, depth), row_feats, ((1,), (1,))
-        ).astype(BF16)
-        line_task = lax.iota(jnp.int32, spread.shape[0]) % (n_tasks * out_rows) // out_rows
-        spread = jnp.where(line_task[:, None] == row_task[None, :], spread, jnp.zeros_like(spread))
-        return dot(spread, back, ((1,), (0,)))
-
-    away = share(1 - core).astype(BF16)
-    mine = share(core) + swapped(away, CORE).astype(F32)
+    away = dot(away_feats, back, ((1,), (0,))).astype(BF16)
+    mine = lax.optimization_barrier(dot(my_feats, back, ((1,), (0,))))
+    mine = mine + swapped(away, CORE).astype(F32)
     blocks = mine.astype(BF16).reshape(n_far, n_tasks * out_rows, width)
+    blocks, query_loss = lax.optimization_barrier((blocks, query_loss))
     arrived = lax.all_to_all(blocks, FAR, 0, 0, tiled=True)
     weight_grad = jnp.sum(arrived.astype(F32), 0).reshape(n_tasks, out_rows, width)
     return (query_loss, weight_grad)

time: 110 us -> 103 us (0.936)
  blocking collectives: 0 us -> 71 us
  waiting for transfers between devices: 64.9 us -> 5.3 us
  starting transfers between devices: 22 us -> 3.35 us
  local copies, waits for them, and re-layouts: 2.94 us -> 1.38 us
  matrix products: 15.2 us -> 16.7 us
    all_to_all x0 -> x2, blocking collectives: none -> 71 us  [the longest x1 38.9 us: per_device(): arrived = lax.all_to_all(blocks, FAR, 0, 0, tiled=True)]
    all_to_all x2 -> x0, waiting for transfers between devices: 51 us -> none  [the longest x1 33.4 us: per_device(): arrived = lax.all_to_all(blocks, FAR, 0, 0, tiled=True)]
    all_to_all x2 -> x0, starting transfers between devices: 18.8 us -> none  [the longest x1 13.7 us: per_device(): lax.all_to_all(jnp.broadcast_to(sent[None], (n_far, *sent.shape)), FAR, 0...]
    ppermute x4, waiting for transfers between devices: 13.9 us -> 5.3 us  [swapped(): return lax.ppermute(x, axis, [(0, 1), (1, 0)])]
    dot_general x13 -> x15, matrix products: 15.2 us -> 16.7 us  [dot(): return lax.dot_general(a, b, (dims, ((), ())), preferred_element_type=F32)]
  transfers between devices with their start and end apart: 6 -> 4, of which waited for: 6 -> 2; matrix products, arithmetic and copies ran while one was open for 3% -> 11% of each run, Pallas kernels for 0% -> 0%
where the time goes in v2:
time: 103 us
  blocking collectives  71 us (69%)
  matrix products  16.7 us (16%)
  waiting for transfers between devices  5.3 us (5%)
  other arithmetic  3.9 us (4%)
  starting transfers between devices  3.35 us (3%)
  local copies, waits for them, and re-layouts  1.38 us (1%)
    all_to_all x1, blocking collectives, per_device(): arrived = lax.all_to_all(blocks, FAR, 0, 0, tiled=True)  38.9 us
    all_to_all x1, blocking collectives, per_device(): lax.all_to_all(jnp.broadcast_to(sent[None], (n_far, *sent.shape)), FAR, 0...  32.2 us
    dot_general x15, matrix products, dot(): return lax.dot_general(a, b, (dims, ((), ())), preferred_element_type=F32)  16.7 us
    ppermute x4, waiting for transfers between devices, swapped(): return lax.ppermute(x, axis, [(0, 1), (1, 0)])  5.3 us
    ppermute x4, starting transfers between devices, swapped(): return lax.ppermute(x, axis, [(0, 1), (1, 0)])  3.35 us
  transfers between devices with their start and end apart: 4, of which 2 were waited for; matrix products, arithmetic and copies ran while one was open for 11% of the time, Pallas kernels for 0%

profile of v2, /device:TPU:2, one launch (start us, length us, event | category | flops | bytes accessed | tf_op | source)
XLA Modules:
  0.0 102.7 jit_solution(17304863403988852313)
XLA Ops:
  0.6 0.0 copy-start
  0.6 0.0 copy-start.1
  0.7 0.7 convert_element_type.104
  1.4 0.1 broadcast_in_dim.121
  1.4 0.7 pad_maximum_fusion.10
  2.1 0.1 broadcast_in_dim.122
  2.3 32.2 %all_to_all.10 = bf16[64,4,896]{2,1,0:T(4,128)(2,1)S(1)} all-to-all(bf16[64,4,896]{2,1,0:T(4,128)(2,1)S(1)} %broadcast_in_dim.122), channel_id=1, replica_groups=mesh['dp_0'=4,'dp_1'=2,'dp_2'=8,'dp_3'=2,'tensor'=2] {'dp_0','dp_1','dp_2'}, dimensions={0} | all-to-all | bytes 917504 | tf_op jit(solution)/shard_map/all_to_all | solution.py:55
  34.4 0.1 reshape.225
  34.6 0.1 collective-permute-start
  34.8 0.0 copy-done
  34.8 0.0 copy-start.2
  34.8 0.0 copy-done.1
  34.8 0.1 fusion.90
  34.9 0.1 broadcast_compare_fusion
  35.1 1.6 %convolution_convert_fusion.5 = bf16[256,384]{1,0:T(8,128)(2,1)S(1)} fusion(bf16[4,768,384]{2,1,0:T(8,128)(2,1)} %param.10, bf16[128,768]{1,0:T(8,128)(2,1)S(1)} %get-tuple-element.46, bf16[128,768]{1,0:T(8,128)(2,1)S(1)} %get-tuple-element.45), kind=kOutput, calls=%fused_computation.30 | convolution fusion | flops 151879680 | bytes 1179648 | tf_op jit(solution)/shard_map/dot_general | solution.py:21
  36.7 0.0 collective-permute-done
  36.7 0.1 constant_dynamic-update-slice_fusion
  36.7 0.1 convert_reduce_fusion.1
  36.9 0.3 fusion.44
  37.2 0.0 copy-done.2
  37.2 0.6 convolution_convert_fusion.1
  37.8 0.2 select_reduce_fusion
  38.0 0.1 slice.92
  38.1 0.4 fusion.15
  38.4 0.4 fusion.14
  38.8 0.4 fusion.35
  39.3 0.6 fusion.10
  39.9 0.6 fusion.9
  40.5 0.7 fusion.16
  41.1 0.3 fusion.91
  41.5 0.1 concatenate.54
  41.6 1.5 %collective-permute-start.1 = (f32[136,512]{1,0:T(8,128)S(1)}, f32[136,512]{1,0:T(8,128)S(1)}, u32[]{:S(2)}, u32[]{:S(2)}) collective-permute-start(f32[136,512]{1,0:T(8,128)S(1)} %concatenate.54), channel_id=1, source_target_pairs={{0,1},{1,0},{2,3},{3,2},{4,5},{5,4},{6,7},{7,6},{8,9},{9,8},{10,11... | collective-permute-start | bytes 835592 | tf_op jit(solution)/shard_map/ppermute | solution.py:17
  43.1 3.8 %compare_select_fusion = bf16[1536,768]{1,0:T(8,128)(2,1)} fusion(s32[1536]{0:T(1024)S(1)} %multiply_add_fusion, s32[768]{0:T(1024)S(1)} %pad_add_fusion, s32[1536]{0:T(1024)S(1)} %get-tuple-element.62, bf16[512,768]{1,0:T(8,128)(2,1)S(1)} %slice.92, bf16[128,768]{1,0:T(8,128)(2,1)S(1)} %get-tuple-element.46, bf16[128,768]{1,0:T(8,128)(2,1)S(1)} %get-tuple-element.45), kind=kOutput, calls=%fused_computation | convolution fusion | flops 1820196864 | bytes 3554304 | tf_op jit(solution)/shard_map/dot_general | solution.py:21
  46.9 0.0 copy-start.3
  46.9 3.8 %compare_select_fusion.1 = bf16[1536,768]{1,0:T(8,128)(2,1)} fusion(s32[1536]{0:T(1024)S(1)} %get-tuple-element.63, s32[768]{0:T(1024)S(1)} %pad_add_fusion, s32[1536]{0:T(1024)S(1)} %get-tuple-element.62, bf16[512,768]{1,0:T(8,128)(2,1)S(1)} %slice.92, bf16[128,768]{1,0:T(8,128)(2,1)S(1)} %get-tuple-element.46, bf16[128,768]{1,0:T(8,128)(2,1)S(1)} %get-tuple-element.45), kind=kOutput, calls=%fused_computation.1 | convolution fusion | flops 1820196864 | bytes 3554304 | tf_op jit(solution)/shard_map/dot_general | solution.py:21
  50.7 0.0 copy-done.3
  50.7 0.1 select_reduce_fusion.2
  50.8 0.0 collective-permute-done.1
  50.8 0.2 select_reduce_fusion.1
  51.1 0.3 fusion.43
  51.3 0.0 copy-start.5
  51.4 1.6 %collective-permute-start.2 = (bf16[136,512]{1,0:T(8,128)(2,1)S(1)}, bf16[136,512]{1,0:T(8,128)(2,1)S(1)}, u32[]{:S(2)}, u32[]{:S(2)}) collective-permute-start(bf16[136,512]{1,0:T(8,128)(2,1)S(1)} %concatenate.58), channel_id=1, source_target_pairs={{0,1},{1,0},{2,3},{3,2},{4,5},{5,4},{6,7},{7,6},{8,9},{9,8},{10,11... | collective-permute-start | bytes 417800 | tf_op jit(solution)/shard_map/ppermute | solution.py:17
  53.1 4.4 %collective-permute-done.2 = bf16[136,512]{1,0:T(8,128)(2,1)S(1)} collective-permute-done((bf16[136,512]{1,0:T(8,128)(2,1)S(1)}, bf16[136,512]{1,0:T(8,128)(2,1)S(1)}, u32[]{:S(2)}, u32[]{:S(2)}) %collective-permute-start.2) | collective-permute-done | bytes 139296 | tf_op jit(solution)/shard_map/ppermute | solution.py:17
  57.6 0.4 fusion.12
  57.9 0.4 fusion.7
  58.4 0.0 copy-done.5
  58.4 0.0 copy-start.4
  58.4 1.4 %convolution_convert_fusion = bf16[1536,384]{1,0:T(8,128)(2,1)S(1)} fusion(bf16[1536,768]{1,0:T(8,128)(2,1)S(1)} %copy-done.5, bf16[512,384]{1,0:T(8,128)(2,1)S(1)} %fusion.7, bf16[256,384]{1,0:T(8,128)(2,1)S(1)} %fusion.12), kind=kOutput, calls=%fused_computation.8 | convolution fusion | flops 907739136 | bytes 4128768 | tf_op jit(solution)/shard_map/dot_general | solution.py:21
  59.8 0.1 collective-permute-start.3
  59.9 0.5 log_subtract_fusion
  60.4 0.0 copy-done.4
  60.4 1.4 %fusion.40 = f32[1536,384]{1,0:T(8,128)S(1)} fusion(bf16[1536,768]{1,0:T(8,128)(2,1)S(1)} %copy-done.4, bf16[512,384]{1,0:T(8,128)(2,1)S(1)} %fusion.7, bf16[256,384]{1,0:T(8,128)(2,1)S(1)} %fusion.12), kind=kOutput, calls=%fused_computation.70 | convolution fusion | flops 907149312 | bytes 5308416 | tf_op jit(solution)/shard_map/dot_general | solution.py:21
  61.8 0.9 collective-permute-done.3
  62.7 0.3 add_convert_fusion
  63.0 38.9 %all_to_all.11 = bf16[64,24,384]{2,1,0:T(8,128)(2,1)S(1)} all-to-all(bf16[64,24,384]{2,1,0:T(8,128)(2,1)S(1)} %bitcast.45), channel_id=1, replica_groups=mesh['dp_0'=4,'dp_1'=2,'dp_2'=8,'dp_3'=2,'tensor'=2] {'dp_0','dp_1','dp_2'}, dimensions={0} | all-to-all | bytes 2359296 | tf_op jit(solution)/shard_map/all_to_all | solution.py:157
  101.9 0.2 convert_reduce_fusion
  102.1 0.6 copy.13
  (28 shorter events, 0.3 us)
Async XLA Ops:
  0.6 34.1 %copy-start = (bf16[256,768]{1,0:T(8,128)(2,1)S(1)}, bf16[256,768]{1,0:T(8,128)(2,1)}, u32[]{:S(2)}) copy-start(bf16[256,768]{1,0:T(8,128)(2,1)} %param.6) | copy-start | bytes 1179652
  0.6 34.2 %copy-start.1 = (s32[256]{0:T(256)S(1)}, s32[256]{0:T(256)}, u32[]{:S(2)}) copy-start(s32[256]{0:T(256)} %param.9) | copy-start | bytes 3076
  34.6 2.1 %collective-permute-start = (bf16[256,896]{1,0:T(8,128)(2,1)S(1)}, bf16[256,896]{1,0:T(8,128)(2,1)S(1)}, u32[]{:S(2)}, u32[]{:S(2)}) collective-permute-start(bf16[256,896]{1,0:T(8,128)(2,1)S(1)} %reshape.225), channel_id=1, source_target_pairs={{0,2},{2,0},{1,3},{3,1},{4,6},{6,4},{5,7},{7,5},{8,10},{10,8},{9,1... | collective-permute-start | bytes 1376264 | tf_op jit(solution)/shard_map/ppermute | solution.py:17
  34.8 2.4 %copy-start.2 = (bf16[4,768,384]{2,1,0:T(8,128)(2,1)S(1)}, bf16[4,768,384]{2,1,0:T(8,128)(2,1)}, u32[]{:S(2)}) copy-start(bf16[4,768,384]{2,1,0:T(8,128)(2,1)} %param.10) | copy-start | bytes 7077892
  41.6 9.2 %collective-permute-start.1 = (f32[136,512]{1,0:T(8,128)S(1)}, f32[136,512]{1,0:T(8,128)S(1)}, u32[]{:S(2)}, u32[]{:S(2)}) collective-permute-start(f32[136,512]{1,0:T(8,128)S(1)} %concatenate.54), channel_id=1, source_target_pairs={{0,1},{1,0},{2,3},{3,2},{4,5},{5,4},{6,7},{7,6},{8,9},{9,8},{10,11... | collective-permute-start | bytes 835592 | tf_op jit(solution)/shard_map/ppermute | solution.py:17
  46.9 3.8 %copy-start.3 = (f32[4]{0:T(128)S(1)}, f32[4]{0:T(128)}, u32[]{:S(2)}) copy-start(f32[4]{0:T(128)} %param.11) | copy-start | bytes 52
  51.3 7.1 %copy-start.5 = (bf16[1536,768]{1,0:T(8,128)(2,1)S(1)}, bf16[1536,768]{1,0:T(8,128)(2,1)}, u32[]{:S(2)}) copy-start(bf16[1536,768]{1,0:T(8,128)(2,1)} %compare_select_fusion.1) | copy-start | bytes 7077892
  51.4 6.1 %collective-permute-start.2 = (bf16[136,512]{1,0:T(8,128)(2,1)S(1)}, bf16[136,512]{1,0:T(8,128)(2,1)S(1)}, u32[]{:S(2)}, u32[]{:S(2)}) collective-permute-start(bf16[136,512]{1,0:T(8,128)(2,1)S(1)} %concatenate.58), channel_id=1, source_target_pairs={{0,1},{1,0},{2,3},{3,2},{4,5},{5,4},{6,7},{7,6},{8,9},{9,8},{10,11... | collective-permute-start | bytes 417800 | tf_op jit(solution)/shard_map/ppermute | solution.py:17
  58.4 2.0 %copy-start.4 = (bf16[1536,768]{1,0:T(8,128)(2,1)S(1)}, bf16[1536,768]{1,0:T(8,128)(2,1)}, u32[]{:S(2)}) copy-start(bf16[1536,768]{1,0:T(8,128)(2,1)} %compare_select_fusion) | copy-start | bytes 7077892
  59.8 2.9 %collective-permute-start.3 = (bf16[1536,384]{1,0:T(8,128)(2,1)S(1)}, bf16[1536,384]{1,0:T(8,128)(2,1)S(1)}, u32[]{:S(2)}, u32[]{:S(2)}) collective-permute-start(bf16[1536,384]{1,0:T(8,128)(2,1)S(1)} %convolution_convert_fusion), channel_id=1, source_target_pairs={{0,2},{2,0},{1,3},{3,1},{4,6},{6,4},{5,7},{7,5},{8,10},{10,8},{9,1... | collective-permute-start | bytes 3538952 | tf_op jit(solution)/shard_map/ppermute | solution.py:17

commit v3 on v2

v3 whole, which is shorter than its diff:
```python
import functools

import jax
import jax.numpy as jnp
from jax import lax
from jax.experimental import pallas as pl
from jax.experimental.pallas import tpu as pltpu
from jax.sharding import Mesh
from jax.sharding import PartitionSpec as P

PLANE = ("dp_0", "dp_1")
LINE = "dp_2"
FAR = PLANE + (LINE,)
CORE = "dp_3"
DP = FAR + (CORE,)
DP_TENSOR = DP + ("tensor",)
EPS = 1e-06
F32 = jnp.float32
BF16 = jnp.bfloat16


def swapped(x, axis):
    return lax.ppermute(x, axis, [(0, 1), (1, 0)])


def dot(a, b, dims):
    return lax.dot_general(a, b, (dims, ((), ())), preferred_element_type=F32)


def lane_dense(column):
    eye = lax.broadcasted_iota(jnp.int32, (128, 128), 0) == lax.broadcasted_iota(
        jnp.int32, (128, 128), 1
    )
    return jnp.concatenate(
        [
            jnp.sum(jnp.where(eye, column[at : at + 128], 0.0), 0, keepdims=True)
            for at in range(0, column.shape[0], 128)
        ],
        1,
    )


def upright(line):
    eye = lax.broadcasted_iota(jnp.int32, (128, 128), 0) == lax.broadcasted_iota(
        jnp.int32, (128, 128), 1
    )
    return jnp.concatenate(
        [
            jnp.sum(jnp.where(eye, line[:, at : at + 128], 0.0), 1, keepdims=True)
            for at in range(0, line.shape[1], 128)
        ],
        0,
    )


def of_own_task(rows, task, weights):
    out = dot(rows, weights[0], ((1,), (0,)))
    for k in range(1, weights.shape[0]):
        out = jnp.where(task == k, dot(rows, weights[k], ((1,), (0,))), out)
    return out.astype(BF16)


def copies_kernel(x, out):
    rows = jnp.concatenate([x[k].astype(F32) for k in range(x.shape[0])]).astype(BF16)
    for k in range(out.shape[0]):
        out[k] = rows


def early_kernel(place, feats, mine, weights, rows, every_out, keys_out):
    depth, own = weights.shape[1], feats.shape[0] // 2
    for at, start in enumerate((place[1], 1 - place[1])):
        rows[at * own : (at + 1) * own] = feats[pl.ds(pl.multiple_of(start * own, own), own), :]
    keys_out[...] = of_own_task(mine[:, :depth], mine[:, depth : depth + 1].astype(F32), weights)
    for k in range(weights.shape[0]):
        every_out[k] = dot(rows[...], weights[k], ((1,), (0,))).astype(BF16)


def equal(a, b):
    return jnp.where(a == b, 1.0, 0.0)


def split(x):
    high = x.astype(BF16)
    rest = x - high.astype(F32)
    middle = rest.astype(BF16)
    return high, middle, (rest - middle.astype(F32)).astype(BF16)


def slots_of(slot, first, count):
    at = lax.broadcasted_iota(jnp.int32, (count, slot.shape[1]), 0) + first
    return equal(at.astype(F32), slot).astype(BF16)


def packed(dots, task, key_task, slot, first, count):
    pick = slots_of(slot, first, count)
    parts = split(jnp.where(task == key_task, dots, 0.0))
    high, middle, low = (dot(pick, part, ((1,), (1,))) for part in parts)
    out = (high + middle) + low
    half = out.shape[1] // 2
    return jnp.concatenate([out[:, half:], out[:, :half]], 1)


def unpacked(slots, slot, first):
    pick = slots_of(slot, first, slots.shape[0])
    high, middle, low = (dot(part, pick, ((0,), (0,))) for part in split(slots))
    return (high + middle) + low


def index_of_keys(place, per, n_keys):
    half = n_keys // 2
    at = lax.broadcasted_iota(jnp.int32, (1, n_keys), 1)
    inside = lax.rem(at, half)
    key_core = jnp.where(at < half, place[0], 1 - place[0])
    return ((2 * lax.div(inside, per) + key_core) * per + lax.rem(inside, per)).astype(F32)


def late_kernel(
    per, place, positive, mine, theirs, mine_proj, every, weights,
    dots_out, message, query_out, keys_out, columns, lines, count_out,
):
    depth, n_query = weights.shape[1], dots_out.shape[0]
    half, own = mine.shape[0], n_query // 2
    keys_out[:half] = mine_proj[...]
    keys_out[half:] = of_own_task(
        theirs[:, :depth], theirs[:, depth : depth + 1].astype(F32), weights
    )
    upright_task = jnp.concatenate(
        [mine[:, depth : depth + 1].astype(F32), theirs[:, depth : depth + 1].astype(F32)]
    )
    key_task = jnp.concatenate(
        [lane_dense(mine[:, depth:].astype(F32)), lane_dense(theirs[:, depth:].astype(F32))], 1
    )
    before = lax.broadcasted_iota(jnp.int32, (2 * half, 2 * half), 0) < lax.broadcasted_iota(
        jnp.int32, (2 * half, 2 * half), 1
    )
    slot = jnp.sum(
        jnp.where(before, equal(upright_task, key_task), 0.0), 0, keepdims=True
    )
    count_out[0] = (jnp.max(slot) + 1.0).astype(jnp.int32)
    line = positive[...].astype(F32)
    pos = upright(
        jnp.where(place[1] == 0, line, jnp.concatenate([line[:, own:], line[:, :own]], 1))
    )
    chosen = pos == index_of_keys(place, per, 2 * half)
    task = jnp.sum(jnp.where(chosen, key_task, 0.0), 1, keepdims=True)
    first = lax.broadcasted_iota(jnp.int32, columns.shape, 1) == 0
    columns[...] = jnp.where(first, task, pos)
    query = every[0].astype(F32)
    for k in range(1, weights.shape[0]):
        query = jnp.where(task == k, every[k].astype(F32), query)
    query_out[...] = query.astype(BF16)
    keys = keys_out[...]
    wide = keys.astype(F32)
    query_sq = lane_dense(jnp.sum(query * query, 1, keepdims=True))
    key_sq = lane_dense(jnp.sum(wide * wide, 1, keepdims=True))
    dots = dot(query_out[...], keys, ((1,), (1,)))
    dots_out[...] = dots
    at = lax.broadcasted_iota(jnp.int32, lines.shape, 0)
    lines[...] = jnp.where(
        at == 0,
        jnp.concatenate([lane_dense(task), key_task], 1),
        jnp.where(
            at == 1,
            jnp.concatenate([query_sq, slot], 1),
            jnp.concatenate([query_sq, key_sq], 1),
        ),
    )
    n_slots = message.shape[0] - 8
    message[:n_slots] = packed(dots, task, key_task, slot, 0, n_slots)
    at = lax.broadcasted_iota(jnp.int32, (8, n_query), 0)
    swapped_sq = jnp.concatenate([query_sq[:, own:], query_sq[:, :own]], 1)
    message[n_slots:] = jnp.where(
        at == 0, swapped_sq, jnp.where(at == 1, key_sq[:, :half], key_sq[:, half:])
    )


def overflow_kernel(n_slots, dots, columns, lines, out):
    n_query = dots.shape[0]
    out[...] = packed(
        dots[...],
        columns[:, :1],
        lines[0:1, n_query:],
        lines[1:2, n_query:],
        n_slots,
        out.shape[0],
    )


def contrast_kernel(
    per, place, count, task_scale, dots, got, over, columns, lines, query_proj, key_proj,
    loss_out, back, full,
):
    n_query, n_keys = dots.shape
    own, n_slots = n_query // 2, got.shape[0] - 8
    task, pos = columns[:, :1], columns[:, 1:2]
    key_task, slot = lines[0:1, n_query:], lines[1:2, n_query:]
    full[...] = dots[...] + unpacked(got[:n_slots], slot, 0)

    @pl.when(count[0] > n_slots)
    def _():
        full[...] += unpacked(over[...], slot, n_slots)

    query_sq = lines[1:2, :n_query] + got[n_slots : n_slots + 1]
    key_sq = lines[2:3, n_query:] + jnp.concatenate(
        [got[n_slots + 1 : n_slots + 2], got[n_slots + 2 : n_slots + 3]], 1
    )
    key_line = 1.0 / jnp.sqrt(key_sq + EPS)
    query_inv, key_inv = upright(1.0 / jnp.sqrt(query_sq + EPS)), upright(key_line)
    scale = jnp.full(task.shape, task_scale[0], F32)
    for k in range(1, task_scale.shape[0]):
        scale = jnp.where(task == k, task_scale[k], scale)
    whole = full[...]
    half_cos = whole * key_line
    scores = half_cos * (scale * query_inv)
    expo = jnp.where(task == key_task, jnp.exp(scores), 0.0)
    chosen = pos == index_of_keys(place, per, n_keys)
    total = jnp.sum(expo, 1, keepdims=True)
    picked = jnp.sum(jnp.where(chosen, scores, 0.0), 1, keepdims=True)
    loss_out[...] = lane_dense((jnp.log(total) - picked)[:own])
    grads = scale * (expo * (1.0 / total) - jnp.where(chosen, 1.0, 0.0))
    grads = grads.astype(BF16)
    wide = grads.astype(F32)
    query_inner = jnp.sum(wide * half_cos, 1, keepdims=True)
    key_inner = upright(jnp.sum(wide * whole * query_inv, 0, keepdims=True))
    query_values, key_values = query_proj[...].astype(F32), key_proj[...].astype(F32)
    query_back = dot(grads, (key_values * key_inv).astype(BF16), ((1,), (0,)))
    key_back = dot(grads, (query_values * query_inv).astype(BF16), ((0,), (0,)))

    def through(values, inverse, grad, inner):
        return (inverse * grad - (inverse * inverse * inverse * inner) * values).astype(BF16)

    back[:n_query] = through(query_values, query_inv, query_back, query_inner)
    back[n_query:] = through(key_values, key_inv, key_back, key_inner)


def spread_kernel(width, n_tasks, place, rows, mine, theirs, task, away, here):
    depth = rows.shape[1]
    half, lines = depth // 2, away.shape[0] // 2
    line = lax.broadcasted_iota(jnp.int32, (lines, 1), 0)
    block = lax.div(line, n_tasks * width)
    r = lax.div(lax.rem(line, n_tasks * width), n_tasks)
    line_task = lax.rem(line, n_tasks).astype(F32)
    same = line_task == task[:1, :]
    for out, core in ((away, 1 - place[0]), (here, place[0])):
        column = (2 * block + core) * width + r
        pick = (column == lax.broadcasted_iota(jnp.int32, (lines, half), 1)).astype(F32).astype(BF16)
        for h in range(2):
            at = 0
            for part in (rows, mine, theirs):
                n = part.shape[0]
                got = dot(pick, part[:, h * half : (h + 1) * half], ((1,), (1,)))
                got = jnp.where(same[:, at : at + n], got, 0.0)
                out[h * lines : (h + 1) * lines, at : at + n] = got.astype(BF16)
                at += n


def in_vmem(n):
    return [pl.BlockSpec(memory_space=pltpu.SMEM)] + [pl.BlockSpec(memory_space=pltpu.VMEM)] * n


SLOTS = 176
ROOM = pltpu.CompilerParams(vmem_limit_bytes=16 << 20)


def cost(flops, moved):
    return pl.CostEstimate(flops=flops, bytes_accessed=moved, transcendentals=0)


def per_device(query_feats, key_feats, key_task, positive, head_weights, task_scale):
    core, member = lax.axis_index(CORE), lax.axis_index("tensor")
    n_tasks, depth, width = head_weights.shape
    n_query = query_feats.shape[0]
    own = n_query // 2
    n_far = lax.axis_size(FAR)
    per = key_feats.shape[0]
    out_rows = depth // (2 * n_far)

    tasks_in = jnp.broadcast_to(key_task.astype(BF16)[:, None], (per, 128))
    sent = jnp.concatenate([key_feats, tasks_in], 1)
    sent = jnp.broadcast_to(sent[None], (lax.axis_size(LINE), *sent.shape))
    place = jnp.stack([core, member])
    sent, place, positive = lax.optimization_barrier((sent, place, positive[None]))
    sent = lax.all_to_all(sent, LINE, 0, 0, tiled=True)
    sent = pl.pallas_call(
        copies_kernel,
        out_shape=jax.ShapeDtypeStruct(
            (lax.axis_size(PLANE), sent.shape[0] * per, depth + 128), BF16
        ),
        in_specs=in_vmem(1)[1:],
        out_specs=in_vmem(1)[1],
        compiler_params=ROOM,
        cost_estimate=cost(1 << 33, 1 << 20),
    )(sent)
    sent = lax.all_to_all(sent, PLANE, 0, 0, tiled=True).reshape(-1, depth + 128)
    arrived = sent
    arrived, place, positive = lax.optimization_barrier((arrived, place, positive))
    theirs = swapped(arrived, CORE)
    n_half = n_far * per
    n_keys = 2 * n_half

    feats, every, mine_proj = pl.pallas_call(
        early_kernel,
        out_shape=(
            jax.ShapeDtypeStruct((n_query, depth), BF16),
            jax.ShapeDtypeStruct((n_tasks, n_query, width), BF16),
            jax.ShapeDtypeStruct((n_half, width), BF16),
        ),
        in_specs=in_vmem(3),
        compiler_params=ROOM,
        out_specs=tuple(in_vmem(3)[1:]),
        cost_estimate=cost(2 * n_tasks * (n_query + n_half) * depth * width, 6 << 20),
    )(place, query_feats, arrived, head_weights)
    dots, message, query_proj, key_proj, columns, lines, count = pl.pallas_call(
        functools.partial(late_kernel, per),
        out_shape=(
            jax.ShapeDtypeStruct((n_query, n_keys), F32),
            jax.ShapeDtypeStruct((SLOTS + 8, n_query), F32),
            jax.ShapeDtypeStruct((n_query, width), BF16),
            jax.ShapeDtypeStruct((n_keys, width), BF16),
            jax.ShapeDtypeStruct((n_query, 128), F32),
            jax.ShapeDtypeStruct((8, n_query + n_keys), F32),
            jax.ShapeDtypeStruct((1,), jnp.int32),
        ),
        in_specs=in_vmem(6),
        out_specs=tuple(in_vmem(6)[1:] + in_vmem(0)),
        compiler_params=ROOM,
        cost_estimate=cost(2 * n_tasks * n_half * depth * width, 6 << 20),
    )(place, positive, arrived, theirs, mine_proj, every, head_weights)
    got = swapped(message, "tensor")

    def follow(operands):
        rest = pl.pallas_call(
            functools.partial(overflow_kernel, SLOTS),
            out_shape=jax.ShapeDtypeStruct((n_keys - SLOTS, n_query), F32),
            in_specs=in_vmem(3)[1:],
            out_specs=in_vmem(1)[1],
            compiler_params=ROOM,
        )(*operands)
        return swapped(rest, "tensor")

    def nothing(operands):
        return jnp.zeros((n_keys - SLOTS, n_query), F32)

    over = lax.cond(count[0] > SLOTS, follow, nothing, (dots, columns, lines))

    n_lines = n_far * n_tasks * out_rows
    away_feats, my_feats = pl.pallas_call(
        functools.partial(spread_kernel, out_rows, n_tasks),
        out_shape=(jax.ShapeDtypeStruct((n_lines, n_query + n_keys), BF16),) * 2,
        in_specs=in_vmem(4),
        out_specs=tuple(in_vmem(2)[1:]),
        compiler_params=ROOM,
        cost_estimate=cost(2 * n_lines * (n_query + n_keys) * depth, 6 << 20),
    )(place, feats, arrived, theirs, lines)
    query_loss, back = pl.pallas_call(
        functools.partial(contrast_kernel, per),
        out_shape=(
            jax.ShapeDtypeStruct((1, own), F32),
            jax.ShapeDtypeStruct((n_query + n_keys, width), BF16),
        ),
        in_specs=in_vmem(0) * 3 + in_vmem(7)[1:],
        out_specs=tuple(in_vmem(2)[1:]),
        scratch_shapes=[pltpu.VMEM((n_query, n_keys), F32)],
        compiler_params=ROOM,
        cost_estimate=cost(20 * n_query * n_keys * width, 6 << 20),
    )(place, count, task_scale, dots, got, over, columns, lines, query_proj, key_proj)
    query_loss = query_loss.reshape(own)

    away = dot(away_feats, back, ((1,), (0,))).astype(BF16)
    mine = lax.optimization_barrier(dot(my_feats, back, ((1,), (0,))))
    mine = mine + swapped(away, CORE).astype(F32)
    n_plane, n_line = lax.axis_size(PLANE), lax.axis_size(LINE)
    blocks = mine.astype(BF16).reshape(n_plane, -1, width)
    blocks, query_loss = lax.optimization_barrier((blocks, query_loss))
    arrived = lax.all_to_all(blocks, PLANE, 0, 0, tiled=True)
    blocks = sum(arrived[k].astype(F32) for k in range(n_plane))
    blocks = blocks.astype(BF16).reshape(n_line, -1, width)
    arrived = lax.all_to_all(blocks, LINE, 0, 0, tiled=True)
    weight_grad = jnp.sum(arrived.astype(F32), 0).reshape(out_rows, n_tasks, width)
    weight_grad = weight_grad.transpose(1, 0, 2)
    return (query_loss, weight_grad)


def solution(mesh):
    split = Mesh(
        mesh.devices.reshape(4, 2, 8, 2, mesh.shape["tensor"]),
        DP_TENSOR,
    )
    return jax.shard_map(
        per_device,
        mesh=split,
        in_specs=(P(DP, None), P(DP, None), P(DP), P(DP), P(None, None, "tensor"), P()),
        out_specs=(P(DP_TENSOR), P(None, DP, "tensor")),
        check_vma=False,
    )
```

time: 103 us -> 89.4 us (0.87)
  matrix products: 16.7 us -> 2.79 us
  Pallas kernels: 0 us -> 11.6 us
  blocking collectives: 71 us -> 65.9 us
  waiting for transfers between devices: 5.3 us -> 2.38 us
  other arithmetic: 3.9 us -> 1.87 us
  starting transfers between devices: 3.35 us -> 1.62 us
    dot_general x15 -> x2, matrix products: 16.7 us -> 2.79 us  [dot(): return lax.dot_general(a, b, (dims, ((), ())), preferred_element_type=F32)]
    pallas_call x0 -> x5, Pallas kernels: none -> 11.6 us  [the longest x1 3.32 us: per_device(): pl.pallas_call(functools.partial(spread_kernel, out_rows, n_tasks), out_s...]
    all_to_all x2 -> x4, blocking collectives: 71 us -> 65.9 us  [the longest x1 21.7 us: per_device(): arrived = lax.all_to_all(blocks, PLANE, 0, 0, tiled=True)]
    ppermute x4 -> x3, waiting for transfers between devices: 5.3 us -> 2.38 us  [swapped(): return lax.ppermute(x, axis, [(0, 1), (1, 0)])]
    ppermute x4 -> x3, starting transfers between devices: 3.35 us -> 1.62 us  [swapped(): return lax.ppermute(x, axis, [(0, 1), (1, 0)])]
  transfers between devices with their start and end apart: 4 -> 3, of which waited for: 2 -> 2; matrix products, arithmetic and copies ran while one was open for 11% -> 2% of each run, Pallas kernels for 0% -> 6%
where the time goes in v3:
time: 89.4 us; the launch traced here: 89.1 us
  blocking collectives  65.9 us (74%)
  Pallas kernels  11.6 us (13%)
  matrix products  2.79 us (3%)
  waiting for transfers between devices  2.38 us (3%)
  other arithmetic  1.87 us (2%)
  starting transfers between devices  1.62 us (2%)
  local copies, waits for them, and re-layouts  1.49 us (2%)
  between operations  1.39 us (2%)
    all_to_all x1, blocking collectives, per_device(): arrived = lax.all_to_all(blocks, PLANE, 0, 0, tiled=True)  21.7 us
    all_to_all x1, blocking collectives, per_device(): sent = lax.all_to_all(sent, LINE, 0, 0, tiled=True)  16.6 us
    all_to_all x1, blocking collectives, per_device(): lax.all_to_all(sent, PLANE, 0, 0, tiled=True).reshape(-1, depth + 128)  16 us
    all_to_all x1, blocking collectives, per_device(): arrived = lax.all_to_all(blocks, LINE, 0, 0, tiled=True)  11.6 us
    pallas_call x1, Pallas kernels, per_device(): pl.pallas_call(functools.partial(spread_kernel, out_rows, n_tasks), out_s...  3.32 us
    pallas_call x1, Pallas kernels, per_device(): pl.pallas_call(functools.partial(contrast_kernel, per), out_shape=(jax.Sh...  3.31 us
    dot_general x2, matrix products, dot(): return lax.dot_general(a, b, (dims, ((), ())), preferred_element_type=F32)  2.79 us
    pallas_call x1, Pallas kernels, per_device(): pl.pallas_call(functools.partial(late_kernel, per), out_shape=(jax.ShapeD...  2.59 us
  transfers between devices with their start and end apart: 3, of which 2 were waited for; matrix products, arithmetic and copies ran while one was open for 2% of the time, Pallas kernels for 6%

profile of v3, /device:TPU:2, one launch (start us, length us, event | category | flops | bytes accessed | tf_op | source)
XLA Modules:
  0.0 89.1 jit_solution(10988106743976796658)
XLA Ops:
  0.6 0.7 convert_element_type.73
  1.3 0.1 pad_add_fusion.place
  1.4 0.1 broadcast_in_dim.6
  1.4 0.7 pad_maximum_fusion
  2.2 16.6 %all_to_all.20.x = bf16[8,4,896]{2,1,0:T(4,128)(2,1)S(1)} all-to-all(bf16[8,4,896]{2,1,0:T(4,128)(2,1)S(1)} %broadcast_in_dim.7), channel_id=1, replica_groups=mesh['dp_0'=4,'dp_1'=2,'dp_2'=8,'dp_3'=2,'tensor'=2] {'dp_2'}, dimensions={0} | all-to-all | bytes 114688 | tf_op jit(solution)/shard_map/all_to_all | solution.py:283
  18.7 0.0 copy-start
  18.7 0.0 copy-start.2
  18.8 16.0 %all_to_all.21 = bf16[8,32,896]{2,1,0:T(8,128)(2,1)S(1)} all-to-all(bf16[8,32,896]{2,1,0:T(8,128)(2,1)S(1)} %shard_map.77), channel_id=1, replica_groups=mesh['dp_0'=4,'dp_1'=2,'dp_2'=8,'dp_3'=2,'tensor'=2] {'dp_0','dp_1'}, dimensions={0} | all-to-all | bytes 917504 | tf_op jit(solution)/shard_map/all_to_all | solution.py:294
  34.7 0.0 copy-start.1
  34.7 0.0 collective-permute-start.1
  34.7 0.0 copy-done
  34.7 0.0 copy-done.2
  34.7 2.4 %shard_map.78 = (bf16[256,768]{1,0:T(8,128)(2,1)S(1)}, bf16[4,256,384]{2,1,0:T(8,128)(2,1)S(1)}, bf16[256,384]{1,0:T(8,128)(2,1)S(1)}) custom-call(s32[2]{0:T(128)S(1)} %pad_add_fusion.place, bf16[256,768]{1,0:T(8,128)(2,1)S(1)} %copy-done.2, bf16[256,896]{1,0:T(8,128)(2,1)S(1)} %bitcast.14, bf16[4,768,384]{2,1,0:T(8,128)(2,1)S(1)} %copy-done), custom_call_target="tpu_custom_call" | custom-call | flops 1207959552 | bytes 6291456 | tf_op jit(solution)/shard_map/pallas_call | solution.py:301
  37.1 0.0 collective-permute-done.1.theirs
  37.2 0.0 copy-done.1
  37.2 2.6 %shard_map.79 = (f32[256,512]{1,0:T(8,128)S(1)}, f32[184,256]{1,0:T(8,128)S(1)}, bf16[256,384]{1,0:T(8,128)(2,1)S(1)}, bf16[512,384]{1,0:T(8,128)(2,1)S(1)}, f32...) custom-call(s32[2]{0:T(128)S(1)} %pad_add_fusion.place, s32[1,256]{1,0:T(1,128)S(1)} %bitcast.17, ...), custom_call_target="tpu_custom_call" | custom-call | flops 603979776 | bytes 6291456 | tf_op jit(solution)/shard_map/pallas_call | solution.py:313
  39.8 1.5 %collective-permute-start.2 = (f32[184,256]{1,0:T(8,128)S(1)}, f32[184,256]{1,0:T(8,128)S(1)}, u32[]{:S(2)}, u32[]{:S(2)}) collective-permute-start(f32[184,256]{1,0:T(8,128)S(1)} %get-tuple-element.49), channel_id=1, source_target_pairs={{0,1},{1,0},{2,3},{3,2},{4,5},{5,4},{6,7},{7,6},{8,9},{9,8},{10,11... | collective-permute-start | bytes 565256 | tf_op jit(solution)/shard_map/ppermute | solution.py:23
  41.9 0.8 conditional.1
  42.0 0.7 broadcast.4
  42.7 0.0 copy-start.3
  42.7 3.3 %shard_map.80 = (bf16[1536,768]{1,0:T(8,128)(2,1)S(1)}, bf16[1536,768]{1,0:T(8,128)(2,1)S(1)}) custom-call(s32[2]{0:T(128)S(1)} %pad_add_fusion.place, bf16[256,768]{1,0:T(8,128)(2,1)S(1)} %get-tuple-element.41.rows, bf16[256,896]{1,0:T(8,128)(2,1)S(1)} %bitcast.16, bf16[256,896]{1,0:T(8,128)(2,1)S(1)} %collective-permute-done.1.theirs, ...), custom_call_target="tpu_custom_call" | custom-call | flops 1811939328 | bytes 6291456 | tf_op jit(solution)/shard_map/pallas_call | solution.py:347
  46.0 0.9 %collective-permute-done.2.got = f32[184,256]{1,0:T(8,128)S(1)} collective-permute-done((f32[184,256]{1,0:T(8,128)S(1)}, f32[184,256]{1,0:T(8,128)S(1)}, u32[]{:S(2)}, u32[]{:S(2)}) %collective-permute-start.2) | collective-permute-done | bytes 188448 | tf_op jit(solution)/shard_map/ppermute | solution.py:23
  47.0 0.0 copy-done.3
  47.0 3.3 %shard_map.81 = (f32[1,128]{1,0:T(1,128)}, bf16[768,384]{1,0:T(8,128)(2,1)S(1)}) custom-call(s32[2]{0:T(128)S(1)} %pad_add_fusion.place, s32[1]{0:T(128)} %get-tuple-element.47.count, f32[4]{0:T(128)S(1)} %copy-done.3, f32[256,512]{1,0:T(8,128)S(1)} %get-tuple-element.48.dots, f32[184,256]{1,0:T(8,128)S(1)} %collective-permute-done.2.got, ...), custom_call_target="tpu_custom_call" | custom-call | flops 1006632960 | bytes 6291456 | tf_op jit(solution)/shard_map/pallas_call | solution.py:355
  50.3 1.4 %convolution_convert_fusion = bf16[1536,384]{1,0:T(8,128)(2,1)S(1)} fusion(bf16[1536,768]{1,0:T(8,128)(2,1)S(1)} %get-tuple-element.54, bf16[768,384]{1,0:T(8,128)(2,1)S(1)} %get-tuple-element.53), kind=kOutput, calls=%fused_computation | convolution fusion | flops 906559488 | bytes 4128768 | tf_op jit(solution)/shard_map/dot_general | solution.py:27
  51.7 0.1 collective-permute-start.3
  51.8 1.4 %fusion = f32[1536,384]{1,0:T(8,128)S(1)} fusion(bf16[1536,768]{1,0:T(8,128)(2,1)S(1)} %get-tuple-element.46, bf16[768,384]{1,0:T(8,128)(2,1)S(1)} %get-tuple-element.53), kind=kOutput, calls=%fused_computation.6 | convolution fusion | flops 905969664 | bytes 5308416 | tf_op jit(solution)/shard_map/dot_general | solution.py:27
  53.2 1.4 %collective-permute-done.3 = bf16[1536,384]{1,0:T(8,128)(2,1)S(1)} collective-permute-done((bf16[1536,384]{1,0:T(8,128)(2,1)S(1)}, bf16[1536,384]{1,0:T(8,128)(2,1)S(1)}, u32[]{:S(2)}, u32[]{:S(2)}) %collective-permute-start.3) | collective-permute-done | bytes 1179680 | tf_op jit(solution)/shard_map/ppermute | solution.py:23
  54.6 0.3 add_convert_fusion
  54.9 21.7 %all_to_all.22 = bf16[8,192,384]{2,1,0:T(8,128)(2,1)S(1)} all-to-all(bf16[8,192,384]{2,1,0:T(8,128)(2,1)S(1)} %bitcast.18), channel_id=1, replica_groups=mesh['dp_0'=4,'dp_1'=2,'dp_2'=8,'dp_3'=2,'tensor'=2] {'dp_0','dp_1'}, dimensions={0} | all-to-all | bytes 2359296 | tf_op jit(solution)/shard_map/all_to_all | solution.py:375
  76.6 0.2 add_convert_fusion.1
  76.8 11.6 %all_to_all.23 = bf16[8,24,384]{2,1,0:T(8,128)(2,1)S(1)} all-to-all(bf16[8,24,384]{2,1,0:T(8,128)(2,1)S(1)} %bitcast.19), channel_id=1, replica_groups=mesh['dp_0'=4,'dp_1'=2,'dp_2'=8,'dp_3'=2,'tensor'=2] {'dp_2'}, dimensions={0} | all-to-all | bytes 294912 | tf_op jit(solution)/shard_map/all_to_all | solution.py:378
  88.4 0.6 reshape.49
  (3 shorter events, 0.1 us)
Async XLA Ops:
  18.7 16.0 %copy-start = (bf16[4,768,384]{2,1,0:T(8,128)(2,1)S(1)}, bf16[4,768,384]{2,1,0:T(8,128)(2,1)}, u32[]{:S(2)}) copy-start(bf16[4,768,384]{2,1,0:T(8,128)(2,1)} %weights.3) | copy-start | bytes 7077892
  18.7 16.0 %copy-start.2 = (bf16[256,768]{1,0:T(8,128)(2,1)S(1)}, bf16[256,768]{1,0:T(8,128)(2,1)}, u32[]{:S(2)}) copy-start(bf16[256,768]{1,0:T(8,128)(2,1)} %feats.1) | copy-start | bytes 1179652
  34.7 2.4 %copy-start.1 = (s32[256]{0:T(256)S(1)}, s32[256]{0:T(256)}, u32[]{:S(2)}) copy-start(s32[256]{0:T(256)} %param.11) | copy-start | bytes 3076
  34.7 2.4 %collective-permute-start.1 = (bf16[256,896]{1,0:T(8,128)(2,1)S(1)}, bf16[256,896]{1,0:T(8,128)(2,1)S(1)}, u32[]{:S(2)}, u32[]{:S(2)}) collective-permute-start(bf16[256,896]{1,0:T(8,128)(2,1)S(1)} %bitcast.13), channel_id=1, source_target_pairs={{0,2},{2,0},{1,3},{3,1},{4,6},{6,4},{5,7},{7,5},{8,10},{10,8},{9,1... | collective-permute-start | bytes 1376264 | tf_op jit(solution)/shard_map/ppermute | solution.py:23
  39.8 7.2 %collective-permute-start.2 = (f32[184,256]{1,0:T(8,128)S(1)}, f32[184,256]{1,0:T(8,128)S(1)}, u32[]{:S(2)}, u32[]{:S(2)}) collective-permute-start(f32[184,256]{1,0:T(8,128)S(1)} %get-tuple-element.49), channel_id=1, source_target_pairs={{0,1},{1,0},{2,3},{3,2},{4,5},{5,4},{6,7},{7,6},{8,9},{9,8},{10,11... | collective-permute-start | bytes 565256 | tf_op jit(solution)/shard_map/ppermute | solution.py:23
  42.7 4.3 %copy-start.3 = (f32[4]{0:T(128)S(1)}, f32[4]{0:T(128)}, u32[]{:S(2)}) copy-start(f32[4]{0:T(128)} %task_scale.1) | copy-start | bytes 52
  51.7 2.9 %collective-permute-start.3 = (bf16[1536,384]{1,0:T(8,128)(2,1)S(1)}, bf16[1536,384]{1,0:T(8,128)(2,1)S(1)}, u32[]{:S(2)}, u32[]{:S(2)}) collective-permute-start(bf16[1536,384]{1,0:T(8,128)(2,1)S(1)} %convolution_convert_fusion), channel_id=1, source_target_pairs={{0,2},{2,0},{1,3},{3,1},{4,6},{6,4},{5,7},{7,5},{8,10},{10,8},{9,1... | collective-permute-start | bytes 3538952 | tf_op jit(solution)/shard_map/ppermute | solution.py:23

commit v4 on v3

--- a/solution.py
+++ b/solution.py
@@ -58,6 +58,14 @@
     for k in range(1, weights.shape[0]):
         out = jnp.where(task == k, dot(rows, weights[k], ((1,), (0,))), out)
     return out.astype(BF16)
+
+
+def task_kernel(task, out):
+    row = lax.broadcasted_iota(jnp.int32, out.shape, 0)
+    tasks = jnp.full(out.shape, task[0], jnp.int32)
+    for k in range(1, out.shape[0]):
+        tasks = jnp.where(row == k, task[k], tasks)
+    out[...] = tasks.astype(F32).astype(BF16)
 
 
 def copies_kernel(x, out):
@@ -258,7 +266,7 @@
     return [pl.BlockSpec(memory_space=pltpu.SMEM)] + [pl.BlockSpec(memory_space=pltpu.VMEM)] * n
 
 
-SLOTS = 176
+SLOTS = 160
 ROOM = pltpu.CompilerParams(vmem_limit_bytes=16 << 20)
 
 
@@ -275,7 +283,14 @@
     per = key_feats.shape[0]
     out_rows = depth // (2 * n_far)
 
-    tasks_in = jnp.broadcast_to(key_task.astype(BF16)[:, None], (per, 128))
+    tasks_in = pl.pallas_call(
+        task_kernel,
+        out_shape=jax.ShapeDtypeStruct((per, 128), BF16),
+        in_specs=in_vmem(0),
+        out_specs=in_vmem(1)[1],
+        compiler_params=ROOM,
+        cost_estimate=cost(1 << 30, 1 << 12),
+    )(key_task)
     sent = jnp.concatenate([key_feats, tasks_in], 1)
     sent = jnp.broadcast_to(sent[None], (lax.axis_size(LINE), *sent.shape))
     place = jnp.stack([core, member])

time: 89.4 us -> 88.9 us (level)
  other arithmetic: 1.87 us -> 0.52 us
where the time goes in v4:
time: 88.9 us; the launch traced here: 88.5 us
  blocking collectives  65.9 us (74%)
  Pallas kernels  12.2 us (14%)
  matrix products  2.79 us (3%)
  local copies, waits for them, and re-layouts  2.07 us (2%)
  waiting for transfers between devices  2.02 us (2%)
  starting transfers between devices  1.62 us (2%)
  between operations  1.42 us (2%)
    all_to_all x1, blocking collectives, per_device(): arrived = lax.all_to_all(blocks, PLANE, 0, 0, tiled=True)  21.7 us
    all_to_all x1, blocking collectives, per_device(): sent = lax.all_to_all(sent, LINE, 0, 0, tiled=True)  16.6 us
    all_to_all x1, blocking collectives, per_device(): lax.all_to_all(sent, PLANE, 0, 0, tiled=True).reshape(-1, depth + 128)  16 us
    all_to_all x1, blocking collectives, per_device(): arrived = lax.all_to_all(blocks, LINE, 0, 0, tiled=True)  11.6 us
    pallas_call x1, Pallas kernels, per_device(): pl.pallas_call(functools.partial(spread_kernel, out_rows, n_tasks), out_s...  3.32 us
    pallas_call x1, Pallas kernels, per_device(): pl.pallas_call(functools.partial(contrast_kernel, per), out_shape=(jax.Sh...  3.31 us
    dot_general x2, matrix products, dot(): return lax.dot_general(a, b, (dims, ((), ())), preferred_element_type=F32)  2.79 us
    pallas_call x1, Pallas kernels, per_device(): pl.pallas_call(functools.partial(late_kernel, per), out_shape=(jax.ShapeD...  2.59 us
  transfers between devices with their start and end apart: 3, of which 2 were waited for; matrix products, arithmetic and copies ran while one was open for 2% of the time, Pallas kernels for 6%

profile of v4, /device:TPU:2, one launch (start us, length us, event | category | flops | bytes accessed | tf_op | source)
XLA Modules:
  0.0 88.5 jit_solution(15342431510039814369)
XLA Ops:
  0.6 0.0 copy-start.5
  0.6 0.0 copy-start.3
  0.7 0.6 copy-done.3
  1.3 0.5 shard_map.77
  1.9 0.1 pad_add_fusion.place
  1.9 0.0 copy-done.5
  2.0 16.6 %all_to_all.20.x = bf16[8,4,896]{2,1,0:T(4,128)(2,1)S(1)} all-to-all(bf16[8,4,896]{2,1,0:T(4,128)(2,1)S(1)} %broadcast_in_dim.4), channel_id=1, replica_groups=mesh['dp_0'=4,'dp_1'=2,'dp_2'=8,'dp_3'=2,'tensor'=2] {'dp_2'}, dimensions={0} | all-to-all | bytes 114688 | tf_op jit(solution)/shard_map/all_to_all | solution.py:298
  18.5 0.0 copy-start
  18.5 0.0 copy-start.2
  18.6 16.0 %all_to_all.21 = bf16[8,32,896]{2,1,0:T(8,128)(2,1)S(1)} all-to-all(bf16[8,32,896]{2,1,0:T(8,128)(2,1)S(1)} %shard_map.78), channel_id=1, replica_groups=mesh['dp_0'=4,'dp_1'=2,'dp_2'=8,'dp_3'=2,'tensor'=2] {'dp_0','dp_1'}, dimensions={0} | all-to-all | bytes 917504 | tf_op jit(solution)/shard_map/all_to_all | solution.py:309
  34.5 0.0 copy-start.1
  34.5 0.0 collective-permute-start.1
  34.5 0.0 copy-done
  34.5 0.0 copy-done.2
  34.6 2.4 %shard_map.79 = (bf16[256,768]{1,0:T(8,128)(2,1)S(1)}, bf16[4,256,384]{2,1,0:T(8,128)(2,1)S(1)}, bf16[256,384]{1,0:T(8,128)(2,1)S(1)}) custom-call(s32[2]{0:T(128)S(1)} %pad_add_fusion.place, bf16[256,768]{1,0:T(8,128)(2,1)S(1)} %copy-done.2, bf16[256,896]{1,0:T(8,128)(2,1)S(1)} %bitcast.14, bf16[4,768,384]{2,1,0:T(8,128)(2,1)S(1)} %copy-done), custom_call_target="tpu_custom_call" | custom-call | flops 1207959552 | bytes 6291456 | tf_op jit(solution)/shard_map/pallas_call | solution.py:316
  37.0 0.0 collective-permute-done.1.theirs
  37.0 0.0 copy-done.1
  37.0 2.6 %shard_map.80 = (f32[256,512]{1,0:T(8,128)S(1)}, f32[168,256]{1,0:T(8,128)S(1)}, bf16[256,384]{1,0:T(8,128)(2,1)S(1)}, bf16[512,384]{1,0:T(8,128)(2,1)S(1)}, f32...) custom-call(s32[2]{0:T(128)S(1)} %pad_add_fusion.place, s32[1,256]{1,0:T(1,128)S(1)} %bitcast.17, ...), custom_call_target="tpu_custom_call" | custom-call | flops 603979776 | bytes 6291456 | tf_op jit(solution)/shard_map/pallas_call | solution.py:328
  39.6 1.5 %collective-permute-start.2 = (f32[168,256]{1,0:T(8,128)S(1)}, f32[168,256]{1,0:T(8,128)S(1)}, u32[]{:S(2)}, u32[]{:S(2)}) collective-permute-start(f32[168,256]{1,0:T(8,128)S(1)} %get-tuple-element.49), channel_id=1, source_target_pairs={{0,1},{1,0},{2,3},{3,2},{4,5},{5,4},{6,7},{7,6},{8,9},{9,8},{10,11... | collective-permute-start | bytes 516104 | tf_op jit(solution)/shard_map/ppermute | solution.py:23
  41.8 0.8 conditional.1
  41.8 0.8 broadcast.3
  42.5 0.0 copy-start.4
  42.5 3.3 %shard_map.81 = (bf16[1536,768]{1,0:T(8,128)(2,1)S(1)}, bf16[1536,768]{1,0:T(8,128)(2,1)S(1)}) custom-call(s32[2]{0:T(128)S(1)} %pad_add_fusion.place, bf16[256,768]{1,0:T(8,128)(2,1)S(1)} %get-tuple-element.41.rows, bf16[256,896]{1,0:T(8,128)(2,1)S(1)} %bitcast.16, bf16[256,896]{1,0:T(8,128)(2,1)S(1)} %collective-permute-done.1.theirs, ...), custom_call_target="tpu_custom_call" | custom-call | flops 1811939328 | bytes 6291456 | tf_op jit(solution)/shard_map/pallas_call | solution.py:362
  45.9 0.6 collective-permute-done.2.got
  46.4 0.0 copy-done.4
  46.4 3.3 %shard_map.82 = (f32[1,128]{1,0:T(1,128)}, bf16[768,384]{1,0:T(8,128)(2,1)S(1)}) custom-call(s32[2]{0:T(128)S(1)} %pad_add_fusion.place, s32[1]{0:T(128)} %get-tuple-element.47.count, f32[4]{0:T(128)S(1)} %copy-done.4, f32[256,512]{1,0:T(8,128)S(1)} %get-tuple-element.48.dots, f32[168,256]{1,0:T(8,128)S(1)} %collective-permute-done.2.got, ...), custom_call_target="tpu_custom_call" | custom-call | flops 1006632960 | bytes 6291456 | tf_op jit(solution)/shard_map/pallas_call | solution.py:370
  49.8 1.4 %convolution_convert_fusion = bf16[1536,384]{1,0:T(8,128)(2,1)S(1)} fusion(bf16[1536,768]{1,0:T(8,128)(2,1)S(1)} %get-tuple-element.54, bf16[768,384]{1,0:T(8,128)(2,1)S(1)} %get-tuple-element.53), kind=kOutput, calls=%fused_computation | convolution fusion | flops 906559488 | bytes 4128768 | tf_op jit(solution)/shard_map/dot_general | solution.py:27
  51.2 0.1 collective-permute-start.3
  51.3 1.4 %fusion = f32[1536,384]{1,0:T(8,128)S(1)} fusion(bf16[1536,768]{1,0:T(8,128)(2,1)S(1)} %get-tuple-element.46, bf16[768,384]{1,0:T(8,128)(2,1)S(1)} %get-tuple-element.53), kind=kOutput, calls=%fused_computation.6 | convolution fusion | flops 905969664 | bytes 5308416 | tf_op jit(solution)/shard_map/dot_general | solution.py:27
  52.7 1.4 %collective-permute-done.3 = bf16[1536,384]{1,0:T(8,128)(2,1)S(1)} collective-permute-done((bf16[1536,384]{1,0:T(8,128)(2,1)S(1)}, bf16[1536,384]{1,0:T(8,128)(2,1)S(1)}, u32[]{:S(2)}, u32[]{:S(2)}) %collective-permute-start.3) | collective-permute-done | bytes 1179680 | tf_op jit(solution)/shard_map/ppermute | solution.py:23
  54.1 0.3 add_convert_fusion
  54.4 21.7 %all_to_all.22 = bf16[8,192,384]{2,1,0:T(8,128)(2,1)S(1)} all-to-all(bf16[8,192,384]{2,1,0:T(8,128)(2,1)S(1)} %bitcast.18), channel_id=1, replica_groups=mesh['dp_0'=4,'dp_1'=2,'dp_2'=8,'dp_3'=2,'tensor'=2] {'dp_0','dp_1'}, dimensions={0} | all-to-all | bytes 2359296 | tf_op jit(solution)/shard_map/all_to_all | solution.py:390
  76.1 0.2 add_convert_fusion.1
  76.2 11.6 %all_to_all.23 = bf16[8,24,384]{2,1,0:T(8,128)(2,1)S(1)} all-to-all(bf16[8,24,384]{2,1,0:T(8,128)(2,1)S(1)} %bitcast.19), channel_id=1, replica_groups=mesh['dp_0'=4,'dp_1'=2,'dp_2'=8,'dp_3'=2,'tensor'=2] {'dp_2'}, dimensions={0} | all-to-all | bytes 294912 | tf_op jit(solution)/shard_map/all_to_all | solution.py:393
  87.9 0.6 reshape.48
  (4 shorter events, 0.1 us)
Async XLA Ops:
  0.6 1.3 %copy-start.5 = (bf16[4,768]{1,0:T(4,128)(2,1)S(1)}, bf16[4,768]{1,0:T(4,128)(2,1)}, u32[]{:S(2)}) copy-start(bf16[4,768]{1,0:T(4,128)(2,1)} %param.9) | copy-start | bytes 18436
  0.6 0.7 copy-start.3
  18.5 16.0 %copy-start = (bf16[4,768,384]{2,1,0:T(8,128)(2,1)S(1)}, bf16[4,768,384]{2,1,0:T(8,128)(2,1)}, u32[]{:S(2)}) copy-start(bf16[4,768,384]{2,1,0:T(8,128)(2,1)} %weights.3) | copy-start | bytes 7077892
  18.5 16.0 %copy-start.2 = (bf16[256,768]{1,0:T(8,128)(2,1)S(1)}, bf16[256,768]{1,0:T(8,128)(2,1)}, u32[]{:S(2)}) copy-start(bf16[256,768]{1,0:T(8,128)(2,1)} %feats.1) | copy-start | bytes 1179652
  34.5 2.4 %copy-start.1 = (s32[256]{0:T(256)S(1)}, s32[256]{0:T(256)}, u32[]{:S(2)}) copy-start(s32[256]{0:T(256)} %param.11) | copy-start | bytes 3076
  34.5 2.4 %collective-permute-start.1 = (bf16[256,896]{1,0:T(8,128)(2,1)S(1)}, bf16[256,896]{1,0:T(8,128)(2,1)S(1)}, u32[]{:S(2)}, u32[]{:S(2)}) collective-permute-start(bf16[256,896]{1,0:T(8,128)(2,1)S(1)} %bitcast.13), channel_id=1, source_target_pairs={{0,2},{2,0},{1,3},{3,1},{4,6},{6,4},{5,7},{7,5},{8,10},{10,8},{9,1... | collective-permute-start | bytes 1376264 | tf_op jit(solution)/shard_map/ppermute | solution.py:23
  39.6 6.9 %collective-permute-start.2 = (f32[168,256]{1,0:T(8,128)S(1)}, f32[168,256]{1,0:T(8,128)S(1)}, u32[]{:S(2)}, u32[]{:S(2)}) collective-permute-start(f32[168,256]{1,0:T(8,128)S(1)} %get-tuple-element.49), channel_id=1, source_target_pairs={{0,1},{1,0},{2,3},{3,2},{4,5},{5,4},{6,7},{7,6},{8,9},{9,8},{10,11... | collective-permute-start | bytes 516104 | tf_op jit(solution)/shard_map/ppermute | solution.py:23
  42.5 3.9 %copy-start.4 = (f32[4]{0:T(128)S(1)}, f32[4]{0:T(128)}, u32[]{:S(2)}) copy-start(f32[4]{0:T(128)} %task_scale.1) | copy-start | bytes 52
  51.2 2.9 %collective-permute-start.3 = (bf16[1536,384]{1,0:T(8,128)(2,1)S(1)}, bf16[1536,384]{1,0:T(8,128)(2,1)S(1)}, u32[]{:S(2)}, u32[]{:S(2)}) collective-permute-start(bf16[1536,384]{1,0:T(8,128)(2,1)S(1)} %convolution_convert_fusion), channel_id=1, source_target_pairs={{0,2},{2,0},{1,3},{3,1},{4,6},{6,4},{5,7},{7,5},{8,10},{10,8},{9,1... | collective-permute-start | bytes 3538952 | tf_op jit(solution)/shard_map/ppermute | solution.py:23

commit v5 on v3

--- a/solution.py
+++ b/solution.py
@@ -94,16 +94,19 @@
 def packed(dots, task, key_task, slot, first, count):
     pick = slots_of(slot, first, count)
     parts = split(jnp.where(task == key_task, dots, 0.0))
-    high, middle, low = (dot(pick, part, ((1,), (1,))) for part in parts)
-    out = (high + middle) + low
+    out = dot(jnp.concatenate([pick] * 3, 1), jnp.concatenate(parts, 1), ((1,), (1,)))
     half = out.shape[1] // 2
     return jnp.concatenate([out[:, half:], out[:, :half]], 1)
 
 
 def unpacked(slots, slot, first):
     pick = slots_of(slot, first, slots.shape[0])
-    high, middle, low = (dot(part, pick, ((0,), (0,))) for part in split(slots))
-    return (high + middle) + low
+    lanes = pl.cdiv(slots.shape[0], 128) * 128 - slots.shape[0]
+    if lanes:
+        slots = jnp.concatenate([slots, jnp.zeros((lanes, slots.shape[1]), F32)])
+        pick = jnp.concatenate([pick, jnp.zeros((lanes, pick.shape[1]), BF16)])
+    parts = jnp.concatenate(split(slots.T), 1)
+    return dot(parts, jnp.concatenate([pick] * 3), ((1,), (0,)))
 
 
 def index_of_keys(place, per, n_keys):

time: 89.4 us -> 89.4 us (level)
  no operation moved by 1% of the time
where the time goes in v5:
time: 89.4 us; the launch traced here: 89.1 us
  blocking collectives  65.9 us (74%)
  Pallas kernels  11.7 us (13%)
  matrix products  2.79 us (3%)
  waiting for transfers between devices  2.38 us (3%)
  other arithmetic  1.87 us (2%)
  starting transfers between devices  1.62 us (2%)
  local copies, waits for them, and re-layouts  1.49 us (2%)
  between operations  1.39 us (2%)
    all_to_all x1, blocking collectives, per_device(): arrived = lax.all_to_all(blocks, PLANE, 0, 0, tiled=True)  21.7 us
    all_to_all x1, blocking collectives, per_device(): sent = lax.all_to_all(sent, LINE, 0, 0, tiled=True)  16.6 us
    all_to_all x1, blocking collectives, per_device(): lax.all_to_all(sent, PLANE, 0, 0, tiled=True).reshape(-1, depth + 128)  16 us
    all_to_all x1, blocking collectives, per_device(): arrived = lax.all_to_all(blocks, LINE, 0, 0, tiled=True)  11.6 us
    pallas_call x1, Pallas kernels, per_device(): pl.pallas_call(functools.partial(contrast_kernel, per), out_shape=(jax.Sh...  3.34 us
    pallas_call x1, Pallas kernels, per_device(): pl.pallas_call(functools.partial(spread_kernel, out_rows, n_tasks), out_s...  3.32 us
    dot_general x2, matrix products, dot(): return lax.dot_general(a, b, (dims, ((), ())), preferred_element_type=F32)  2.79 us
    pallas_call x1, Pallas kernels, per_device(): pl.pallas_call(functools.partial(late_kernel, per), out_shape=(jax.ShapeD...  2.58 us
  transfers between devices with their start and end apart: 3, of which 2 were waited for; matrix products, arithmetic and copies ran while one was open for 2% of the time, Pallas kernels for 6%

profile of v5, /device:TPU:2, one launch (start us, length us, event | category | flops | bytes accessed | tf_op | source)
XLA Modules:
  0.0 89.1 jit_solution(10836364670591288845)
XLA Ops:
  0.6 0.7 convert_element_type.73
  1.3 0.1 pad_add_fusion.place
  1.4 0.1 broadcast_in_dim.6
  1.4 0.7 pad_maximum_fusion
  2.2 16.6 %all_to_all.20.x = bf16[8,4,896]{2,1,0:T(4,128)(2,1)S(1)} all-to-all(bf16[8,4,896]{2,1,0:T(4,128)(2,1)S(1)} %broadcast_in_dim.7), channel_id=1, replica_groups=mesh['dp_0'=4,'dp_1'=2,'dp_2'=8,'dp_3'=2,'tensor'=2] {'dp_2'}, dimensions={0} | all-to-all | bytes 114688 | tf_op jit(solution)/shard_map/all_to_all | solution.py:286
  18.7 0.0 copy-start
  18.7 0.0 copy-start.2
  18.8 16.0 %all_to_all.21 = bf16[8,32,896]{2,1,0:T(8,128)(2,1)S(1)} all-to-all(bf16[8,32,896]{2,1,0:T(8,128)(2,1)S(1)} %shard_map.77), channel_id=1, replica_groups=mesh['dp_0'=4,'dp_1'=2,'dp_2'=8,'dp_3'=2,'tensor'=2] {'dp_0','dp_1'}, dimensions={0} | all-to-all | bytes 917504 | tf_op jit(solution)/shard_map/all_to_all | solution.py:297
  34.7 0.0 copy-start.1
  34.7 0.0 collective-permute-start.1
  34.7 0.0 copy-done
  34.7 0.0 copy-done.2
  34.7 2.4 %shard_map.78 = (bf16[256,768]{1,0:T(8,128)(2,1)S(1)}, bf16[4,256,384]{2,1,0:T(8,128)(2,1)S(1)}, bf16[256,384]{1,0:T(8,128)(2,1)S(1)}) custom-call(s32[2]{0:T(128)S(1)} %pad_add_fusion.place, bf16[256,768]{1,0:T(8,128)(2,1)S(1)} %copy-done.2, bf16[256,896]{1,0:T(8,128)(2,1)S(1)} %bitcast.14, bf16[4,768,384]{2,1,0:T(8,128)(2,1)S(1)} %copy-done), custom_call_target="tpu_custom_call" | custom-call | flops 1207959552 | bytes 6291456 | tf_op jit(solution)/shard_map/pallas_call | solution.py:304
  37.1 0.0 collective-permute-done.1.theirs
  37.2 0.0 copy-done.1
  37.2 2.6 %shard_map.79 = (f32[256,512]{1,0:T(8,128)S(1)}, f32[184,256]{1,0:T(8,128)S(1)}, bf16[256,384]{1,0:T(8,128)(2,1)S(1)}, bf16[512,384]{1,0:T(8,128)(2,1)S(1)}, f32...) custom-call(s32[2]{0:T(128)S(1)} %pad_add_fusion.place, s32[1,256]{1,0:T(1,128)S(1)} %bitcast.17, ...), custom_call_target="tpu_custom_call" | custom-call | flops 603979776 | bytes 6291456 | tf_op jit(solution)/shard_map/pallas_call | solution.py:316
  39.8 1.5 %collective-permute-start.2 = (f32[184,256]{1,0:T(8,128)S(1)}, f32[184,256]{1,0:T(8,128)S(1)}, u32[]{:S(2)}, u32[]{:S(2)}) collective-permute-start(f32[184,256]{1,0:T(8,128)S(1)} %get-tuple-element.49), channel_id=1, source_target_pairs={{0,1},{1,0},{2,3},{3,2},{4,5},{5,4},{6,7},{7,6},{8,9},{9,8},{10,11... | collective-permute-start | bytes 565256 | tf_op jit(solution)/shard_map/ppermute | solution.py:23
  41.9 0.8 conditional.1
  41.9 0.7 broadcast.4
  42.7 0.0 copy-start.3
  42.7 3.3 %shard_map.80 = (bf16[1536,768]{1,0:T(8,128)(2,1)S(1)}, bf16[1536,768]{1,0:T(8,128)(2,1)S(1)}) custom-call(s32[2]{0:T(128)S(1)} %pad_add_fusion.place, bf16[256,768]{1,0:T(8,128)(2,1)S(1)} %get-tuple-element.41.rows, bf16[256,896]{1,0:T(8,128)(2,1)S(1)} %bitcast.16, bf16[256,896]{1,0:T(8,128)(2,1)S(1)} %collective-permute-done.1.theirs, ...), custom_call_target="tpu_custom_call" | custom-call | flops 1811939328 | bytes 6291456 | tf_op jit(solution)/shard_map/pallas_call | solution.py:350
  46.0 0.9 %collective-permute-done.2.got = f32[184,256]{1,0:T(8,128)S(1)} collective-permute-done((f32[184,256]{1,0:T(8,128)S(1)}, f32[184,256]{1,0:T(8,128)S(1)}, u32[]{:S(2)}, u32[]{:S(2)}) %collective-permute-start.2) | collective-permute-done | bytes 188448 | tf_op jit(solution)/shard_map/ppermute | solution.py:23
  47.0 0.0 copy-done.3
  47.0 3.3 %shard_map.81 = (f32[1,128]{1,0:T(1,128)}, bf16[768,384]{1,0:T(8,128)(2,1)S(1)}) custom-call(s32[2]{0:T(128)S(1)} %pad_add_fusion.place, s32[1]{0:T(128)} %get-tuple-element.47.count, f32[4]{0:T(128)S(1)} %copy-done.3, f32[256,512]{1,0:T(8,128)S(1)} %get-tuple-element.48.dots, f32[184,256]{1,0:T(8,128)S(1)} %collective-permute-done.2.got, ...), custom_call_target="tpu_custom_call" | custom-call | flops 1006632960 | bytes 6291456 | tf_op jit(solution)/shard_map/pallas_call | solution.py:358
  50.3 1.4 %convolution_convert_fusion = bf16[1536,384]{1,0:T(8,128)(2,1)S(1)} fusion(bf16[1536,768]{1,0:T(8,128)(2,1)S(1)} %get-tuple-element.54, bf16[768,384]{1,0:T(8,128)(2,1)S(1)} %get-tuple-element.53), kind=kOutput, calls=%fused_computation | convolution fusion | flops 906559488 | bytes 4128768 | tf_op jit(solution)/shard_map/dot_general | solution.py:27
  51.7 0.1 collective-permute-start.3
  51.8 1.4 %fusion = f32[1536,384]{1,0:T(8,128)S(1)} fusion(bf16[1536,768]{1,0:T(8,128)(2,1)S(1)} %get-tuple-element.46, bf16[768,384]{1,0:T(8,128)(2,1)S(1)} %get-tuple-element.53), kind=kOutput, calls=%fused_computation.6 | convolution fusion | flops 905969664 | bytes 5308416 | tf_op jit(solution)/shard_map/dot_general | solution.py:27
  53.2 1.4 %collective-permute-done.3 = bf16[1536,384]{1,0:T(8,128)(2,1)S(1)} collective-permute-done((bf16[1536,384]{1,0:T(8,128)(2,1)S(1)}, bf16[1536,384]{1,0:T(8,128)(2,1)S(1)}, u32[]{:S(2)}, u32[]{:S(2)}) %collective-permute-start.3) | collective-permute-done | bytes 1179680 | tf_op jit(solution)/shard_map/ppermute | solution.py:23
  54.7 0.3 add_convert_fusion
  54.9 21.7 %all_to_all.22 = bf16[8,192,384]{2,1,0:T(8,128)(2,1)S(1)} all-to-all(bf16[8,192,384]{2,1,0:T(8,128)(2,1)S(1)} %bitcast.18), channel_id=1, replica_groups=mesh['dp_0'=4,'dp_1'=2,'dp_2'=8,'dp_3'=2,'tensor'=2] {'dp_0','dp_1'}, dimensions={0} | all-to-all | bytes 2359296 | tf_op jit(solution)/shard_map/all_to_all | solution.py:378
  76.6 0.2 add_convert_fusion.1
  76.8 11.6 %all_to_all.23 = bf16[8,24,384]{2,1,0:T(8,128)(2,1)S(1)} all-to-all(bf16[8,24,384]{2,1,0:T(8,128)(2,1)S(1)} %bitcast.19), channel_id=1, replica_groups=mesh['dp_0'=4,'dp_1'=2,'dp_2'=8,'dp_3'=2,'tensor'=2] {'dp_2'}, dimensions={0} | all-to-all | bytes 294912 | tf_op jit(solution)/shard_map/all_to_all | solution.py:381
  88.5 0.6 reshape.49
  (3 shorter events, 0.1 us)
Async XLA Ops:
  18.7 16.0 %copy-start = (bf16[4,768,384]{2,1,0:T(8,128)(2,1)S(1)}, bf16[4,768,384]{2,1,0:T(8,128)(2,1)}, u32[]{:S(2)}) copy-start(bf16[4,768,384]{2,1,0:T(8,128)(2,1)} %weights.3) | copy-start | bytes 7077892
  18.7 16.0 %copy-start.2 = (bf16[256,768]{1,0:T(8,128)(2,1)S(1)}, bf16[256,768]{1,0:T(8,128)(2,1)}, u32[]{:S(2)}) copy-start(bf16[256,768]{1,0:T(8,128)(2,1)} %feats.1) | copy-start | bytes 1179652
  34.7 2.4 %copy-start.1 = (s32[256]{0:T(256)S(1)}, s32[256]{0:T(256)}, u32[]{:S(2)}) copy-start(s32[256]{0:T(256)} %param.11) | copy-start | bytes 3076
  34.7 2.4 %collective-permute-start.1 = (bf16[256,896]{1,0:T(8,128)(2,1)S(1)}, bf16[256,896]{1,0:T(8,128)(2,1)S(1)}, u32[]{:S(2)}, u32[]{:S(2)}) collective-permute-start(bf16[256,896]{1,0:T(8,128)(2,1)S(1)} %bitcast.13), channel_id=1, source_target_pairs={{0,2},{2,0},{1,3},{3,1},{4,6},{6,4},{5,7},{7,5},{8,10},{10,8},{9,1... | collective-permute-start | bytes 1376264 | tf_op jit(solution)/shard_map/ppermute | solution.py:23
  39.8 7.2 %collective-permute-start.2 = (f32[184,256]{1,0:T(8,128)S(1)}, f32[184,256]{1,0:T(8,128)S(1)}, u32[]{:S(2)}, u32[]{:S(2)}) collective-permute-start(f32[184,256]{1,0:T(8,128)S(1)} %get-tuple-element.49), channel_id=1, source_target_pairs={{0,1},{1,0},{2,3},{3,2},{4,5},{5,4},{6,7},{7,6},{8,9},{9,8},{10,11... | collective-permute-start | bytes 565256 | tf_op jit(solution)/shard_map/ppermute | solution.py:23
  42.7 4.3 %copy-start.3 = (f32[4]{0:T(128)S(1)}, f32[4]{0:T(128)}, u32[]{:S(2)}) copy-start(f32[4]{0:T(128)} %task_scale.1) | copy-start | bytes 52
  51.7 2.9 %collective-permute-start.3 = (bf16[1536,384]{1,0:T(8,128)(2,1)S(1)}, bf16[1536,384]{1,0:T(8,128)(2,1)S(1)}, u32[]{:S(2)}, u32[]{:S(2)}) collective-permute-start(bf16[1536,384]{1,0:T(8,128)(2,1)S(1)} %convolution_convert_fusion), channel_id=1, source_target_pairs={{0,2},{2,0},{1,3},{3,1},{4,6},{6,4},{5,7},{7,5},{8,10},{10,8},{9,1... | collective-permute-start | bytes 3538952 | tf_op jit(solution)/shard_map/ppermute | solution.py:23
